TPU v7x, 128 devices: a whole 4x4x4 slice. The times are simulated.
128 devices in a mesh: model: 16 (over z, y), data: 8 (over x, core).
Axes of the slice: x: 4, y: 4, z: 4, core: 2. Of those that a mesh axis runs over, the one named last changes fastest.
Arguments:
- h_a: bfloat16 [16384, 2048], P('data')
- h_b: bfloat16 [16384, 2048], P('data')
- w_one: bfloat16 [2048, 2048], P(None, 'model')
- w_two: bfloat16 [2048, 2048], P('model')
- w_three: bfloat16 [2048, 2048], P(None, 'model')
- g_one: float32 [2048], P('model')
- b_one: float32 [2048], P('model')
- g_two: float32 [2048], replicated
- b_two: float32 [2048], replicated
- lam_off: float32 [1], replicated
Outputs:
- output 1: float32 [1], replicated
- output 2: float32 [2048, 2048], P(None, 'model')
- output 3: float32 [2048, 2048], P('model')
- output 4: float32 [2048, 2048], P(None, 'model')
- output 5: float32 [2048], P('model')
- output 6: float32 [2048], P('model')
- output 7: float32 [2048], replicated
- output 8: float32 [2048], replicated
All inputs are finite; a program needn't handle non-finite values.
Results may differ from a plain program's by a relative error of at most 0.001.
Values are sent between devices in bfloat16 or wider.
A program may use at most 1 GiB of HBM per device.

v0:
```python
import jax
import jax.numpy as jnp
from jax import lax
from jax.sharding import PartitionSpec as P

BN_EPS = 1e-5


def batch_norm(pre_act, total_rows):
    local_sums = jnp.stack([jnp.sum(pre_act, axis=1, keepdims=True), jnp.sum(pre_act * pre_act, axis=1, keepdims=True)])
    moments = lax.psum(local_sums, 'data') / total_rows
    inv_std = lax.rsqrt(moments[1] - moments[0] * moments[0] + BN_EPS)
    return (pre_act - moments[0]) * inv_std, inv_std


def bn_backward(d_act, lin_val, norm_val, inv_std, gamma_vec, total_rows):
    d_lin = jnp.where(lin_val > 0, d_act, 0.0)
    local_sums = jnp.stack([jnp.sum(d_lin, axis=1, keepdims=True), jnp.sum(d_lin * norm_val, axis=1, keepdims=True)])
    global_sums = lax.psum(local_sums, 'data')
    d_pre = gamma_vec * inv_std * (d_lin - (global_sums[0] + norm_val * global_sums[1]) / total_rows)
    return d_pre.astype(jnp.bfloat16), jnp.sum(global_sums[1], axis=(0, 1)), jnp.sum(global_sums[0], axis=(0, 1))


def solution(mesh):
    data_size = mesh.shape['data']

    def shard_body(h_a, h_b, w_one, w_two, w_three, g_one, b_one, g_two, b_two, lam_off):
        local_rows = h_a.shape[0]
        total_rows = local_rows * data_size
        full_dim, feat_dev = w_three.shape
        view_feats = jnp.stack([h_a, h_b])
        pre_one = jnp.einsum('vnf,fd->vnd', view_feats, w_one, preferred_element_type=jnp.float32)
        norm_one, inv_one = batch_norm(pre_one, total_rows)
        lin_one = g_one * norm_one + b_one
        act_one = jnp.maximum(lin_one, 0.0).astype(jnp.bfloat16)
        pre_two = lax.psum(jnp.einsum('woe,ef->wof', act_one, w_two, preferred_element_type=jnp.float32), 'model')
        norm_two, inv_two = batch_norm(pre_two, total_rows)
        lin_two = g_two * norm_two + b_two
        act_two = jnp.maximum(lin_two, 0.0).astype(jnp.bfloat16)
        pre_out = jnp.einsum('woe,ef->wof', act_two, w_three, preferred_element_type=jnp.float32)
        norm_out, inv_out = batch_norm(pre_out, total_rows)
        embed_bf = norm_out.astype(jnp.bfloat16)
        emb_b_full = lax.all_gather(embed_bf[1], 'model', axis=1, tiled=True)
        corr_part = jnp.einsum('ni,nj->ij', embed_bf[0], emb_b_full, preferred_element_type=jnp.float32)
        corr_mat = lax.psum(corr_part, 'data') / total_rows
        row_ids = lax.axis_index('model') * feat_dev + lax.broadcasted_iota(jnp.int32, (feat_dev, 1), 0)
        col_ids = lax.broadcasted_iota(jnp.int32, (1, full_dim), 1)
        is_diag = row_ids == col_ids
        lam_val = lam_off[0]
        loss_part = jnp.sum(jnp.where(is_diag, (1.0 - corr_mat) * (1.0 - corr_mat), lam_val * corr_mat * corr_mat))
        loss_val = lax.psum(loss_part, 'model')
        grad_c = jnp.where(is_diag, -2.0 * (1.0 - corr_mat), 2.0 * lam_val * corr_mat).astype(jnp.bfloat16)
        d_emb_a = jnp.einsum('nj,ij->ni', emb_b_full, grad_c, preferred_element_type=jnp.float32)
        d_part_b = jnp.einsum('ni,ij->nj', embed_bf[0], grad_c, preferred_element_type=jnp.float32)
        d_emb_b = lax.psum_scatter(d_part_b, 'model', scatter_dimension=1, tiled=True)
        d_emb = jnp.stack([d_emb_a, d_emb_b]) / total_rows
        embed_f = embed_bf.astype(jnp.float32)
        grad_sums = jnp.stack([jnp.sum(d_emb, axis=1, keepdims=True), jnp.sum(d_emb * embed_f, axis=1, keepdims=True)])
        grad_moments = lax.psum(grad_sums, 'data') / total_rows
        d_out = (inv_out * (d_emb - grad_moments[0] - embed_f * grad_moments[1])).astype(jnp.bfloat16)
        dw_three = lax.psum(jnp.einsum('woe,wof->ef', act_two, d_out, preferred_element_type=jnp.float32), 'data')
        d_act_two = lax.psum(jnp.einsum('wof,ef->woe', d_out, w_three, preferred_element_type=jnp.float32), 'model')
        d_pre_two, dg_two, db_two = bn_backward(d_act_two, lin_two, norm_two, inv_two, g_two, total_rows)
        dw_two = lax.psum(jnp.einsum('woe,wof->ef', act_one, d_pre_two, preferred_element_type=jnp.float32), 'data')
        d_act_one = jnp.einsum('wof,ef->woe', d_pre_two, w_two, preferred_element_type=jnp.float32)
        d_pre_one, dg_one, db_one = bn_backward(d_act_one, lin_one, norm_one, inv_one, g_one, total_rows)
        dw_one = lax.psum(jnp.einsum('vnf,vnd->fd', view_feats, d_pre_one, preferred_element_type=jnp.float32), 'data')
        return loss_val.reshape(1), dw_one, dw_two, dw_three, dg_one, db_one, dg_two, db_two

    in_specs = (P('data', None), P('data', None), P(None, 'model'), P('model', None), P(None, 'model'),
                P('model'), P('model'), P(), P(), P())
    out_specs = (P(), P(None, 'model'), P('model', None), P(None, 'model'), P('model'), P('model'), P(), P())
    return jax.shard_map(shard_body, mesh=mesh, in_specs=in_specs, out_specs=out_specs, check_vma=False)
```

profile of v0, /device:TPU:1, one launch (start us, length us, event | category | flops | bytes accessed | tf_op | source)
XLA Modules:
  0.0 1379.9 jit_solution(17963052735755703350)
XLA Ops:
  7.3 8.7 fusion.48
  16.0 13.2 psum.91
  29.2 0.5 fusion.41
  29.8 13.0 fusion.27
  42.9 0.0 all-gather.3.cloned.1.call-start
  42.9 392.0 %all-reduce.6.cloned.1.call-done = f32[2,2048,2048]{2,1,0:T(8,128)} async-done(((f32[2,2048,2048]{2,1,0:T(8,128)}), f32[2,2048,2048]{2,1,0:T(8,128)}) %all-reduce.6.cloned.1.call-update) | async-done | bytes 33554448 | tf_op jit(solution)/shard_map/psum | solution.py:36
  435.0 12.8 fusion.45
  447.8 22.7 %psum.93 = f32[2,2,1,2048]{3,1,2,0:T(2,128)S(1)} all-reduce(f32[2,2,1,2048]{3,1,2,0:T(2,128)S(1)} %pad_maximum_fusion.5), channel_id=1, replica_groups=mesh['model'=16,'data'=8] {'data'}, use_global_device_ids=true, to_apply=%region_6.0 | all-reduce | flops 8192 | bytes 65536 | tf_op jit(solution)/shard_map/psum | solution.py:11
  470.6 14.0 %fusion.47 = (f32[2,128]{1,0:T(2,128)S(1)}, f32[2,128]{1,0:T(2,128)S(1)}, f32[2,2048,128]{2,1,0:T(8,128)S(1)}) fusion(bf16[2048,128]{1,0:T(8,128)(2,1)S(1)} %copy-done, f32[2,2048,2048]{2,1,0:T(8,128)} %all-reduce.6.cloned.1.call-done, f32[2048]{0:T(1024)S(1)} %copy-done.11, f32[2,2048]{1,0:T(2,128)S(1)} %get-tuple-element.30, ...), kind=kOutput, calls=%fused_computation.98 | convolution fusion | flops 2199387648 | bytes 36227072 | tf_op jit(solution)/shard_map/woe,ef->wof/dot_general | solution.py:40
  484.6 15.3 %psum.94 = f32[2,2,1,128]{3,1,2,0:T(2,128)S(1)} all-reduce(f32[2,2,1,128]{3,1,2,0:T(2,128)S(1)} %pad_maximum_fusion.8), channel_id=1, replica_groups=mesh['model'=16,'data'=8] {'data'}, use_global_device_ids=true, to_apply=%region_9.0 | all-reduce | flops 512 | bytes 4096 | tf_op jit(solution)/shard_map/psum | solution.py:11
  499.9 0.2 multiply_convert_fusion.2
  500.2 1.0 copy-done.7
  501.2 0.8 slice.74
  502.0 0.0 all-reduce.8.cloned.1.call-start
  502.1 72.7 %all-gather.3.cloned.1.call-done = bf16[1,2048,2048]{2,1,0:T(8,128)(2,1)} async-done(((bf16[1,2048,128]{2,1,0:T(8,128)(2,1)}), bf16[1,2048,2048]{2,1,0:T(8,128)(2,1)}) %all-gather.3.cloned.1.call-update) | async-done | bytes 8388624 | tf_op jit(solution)/shard_map/all_gather | solution.py:43
  574.8 5.8 fusion.5
  580.6 0.5 reduce-scatter.2.cloned.1.call-start
  581.8 60.0 %all-reduce.8.cloned.1.call-done = f32[128,2048]{1,0:T(8,128)} async-done(((f32[128,2048]{1,0:T(8,128)}), f32[128,2048]{1,0:T(8,128)}) %all-reduce.8.cloned.1.call-update) | async-done | bytes 1048592 | tf_op jit(solution)/shard_map/psum | solution.py:45
  641.8 9.5 fusion.30
  651.3 0.0 all-reduce.10.cloned.1.call-start
  651.4 7.0 fusion.7
  658.4 104.5 %reduce-scatter.2.cloned.1.call-done = f32[2048,128]{1,0:T(8,128)} async-done(((f32[2048,2048]{1,0:T(8,128)}), f32[2048,128]{1,0:T(8,128)}) %reduce-scatter.2.cloned.1.call-update) | async-done | bytes 1048592 | tf_op jit(solution)/shard_map/reduce_scatter | solution.py:55
  762.9 2.0 fusion.15
  764.8 13.3 psum.97
  778.2 2.1 fusion.14
  780.3 1.0 copy-done.5
  781.3 13.1 fusion.22
  794.4 0.0 all-reduce.12.cloned.1.call-start
  794.4 1.1 copy-done.6
  795.6 14.7 %convolution_bitcast_fusion.1 = f32[2048,128]{1,0:T(8,128)} fusion(bf16[2,2048,128]{2,1,0:T(8,128)(2,1)S(1)} %copy-done.6, f32[2,2048,2048]{2,1,0:T(8,128)} %all-reduce.6.cloned.1.call-done, f32[2048]{0:T(1024)S(1)} %copy-done.11, f32[2,2048]{1,0:T(2,128)S(1)} %get-tuple-element.30, f32[2,2048]{1,0:T(2,128)S(1)} %slice_bitcast_fusion.4, f32[2048]{0:T(1024)S(1)} %copy-done.10), kind=kOutput, calls=%fused_computation.21 | convolution fusion | flops 2197815296 | bytes 35700736 | tf_op jit(solution)/shard_map/woe,wof->ef/dot_general | solution.py:61
  810.3 372.7 %all-reduce.10.cloned.1.call-done = f32[2,2048,2048]{2,1,0:T(8,128)} async-done(((f32[2,2048,2048]{2,1,0:T(8,128)}), f32[2,2048,2048]{2,1,0:T(8,128)}) %all-reduce.10.cloned.1.call-update) | async-done | bytes 33554448 | tf_op jit(solution)/shard_map/psum | solution.py:62
  1183.0 22.0 %fusion.2 = (f32[2,2048]{1,0:T(2,128)S(1)}, f32[2,2048]{1,0:T(2,128)S(1)}) fusion(f32[2,2048,2048]{2,1,0:T(8,128)} %all-reduce.10.cloned.1.call-done, f32[2048]{0:T(1024)S(1)} %copy-done.11, f32[2,2048]{1,0:T(2,128)S(1)} %get-tuple-element.30, f32[2,2048,2048]{2,1,0:T(8,128)} %all-reduce.6.cloned.1.call-done, f32[2,2048]{1,0:T(2,128)S(1)} %slice_bitcast_fusion.4, ...), kind=kLoop, calls=%fused_computation.10 | loop fusion | flops 75489280 | bytes 67190784 | tf_op jit(solution)/shard_map/reduce_sum | solution.py:18
  1205.0 23.0 %psum.99 = f32[2,2,1,2048]{3,1,2,0:T(2,128)S(1)} all-reduce(f32[2,2,1,2048]{3,1,2,0:T(2,128)S(1)} %pad_maximum_fusion.6), channel_id=1, replica_groups=mesh['model'=16,'data'=8] {'data'}, use_global_device_ids=true, to_apply=%region_20.21 | all-reduce | flops 8192 | bytes 65536 | tf_op jit(solution)/shard_map/psum | solution.py:19
  1228.0 0.6 slice_reduce_fusion.1
  1228.6 29.1 %multiply_convert_fusion = bf16[2,2048,2048]{2,1,0:T(8,128)(2,1)} fusion(f32[2,2048,2048]{2,1,0:T(8,128)} %all-reduce.6.cloned.1.call-done, f32[2,2048]{1,0:T(2,128)S(1)} %get-tuple-element.27, f32[2,2048]{1,0:T(2,128)S(1)} %get-tuple-element.28, f32[2,2048]{1,0:T(2,128)S(1)} %get-tuple-element.29, f32[2,2048]{1,0:T(2,128)S(1)} %get-tuple-element.30, ...), kind=kLoop, calls=%fused_computation | loop fusion | flops 100663296 | bytes 83984384 | tf_op jit(solution)/shard_map/convert_element_type | solution.py:21
  1257.7 9.3 convolution_bitcast_fusion
  1267.0 1.6 copy-done.2
  1268.6 0.0 copy-done.9
  1268.7 6.1 fusion.46
  1274.8 15.5 %psum.100 = f32[2,2,1,128]{3,1,2,0:T(2,128)S(1)} all-reduce(f32[2,2,1,128]{3,1,2,0:T(2,128)S(1)} %pad_maximum_fusion.10), channel_id=1, replica_groups=mesh['model'=16,'data'=8] {'data'}, use_global_device_ids=true, to_apply=%region_23.24 | all-reduce | flops 512 | bytes 4096 | tf_op jit(solution)/shard_map/psum | solution.py:19
  1290.4 0.5 slice_reduce_fusion.3
  1290.9 10.1 fusion.10
  1301.0 2.1 select_reduce_fusion
  1303.1 33.0 %psum.96 = f32[1]{0:T(128)} all-reduce(f32[1]{0:T(128)} %bitcast.20), channel_id=1, replica_groups=mesh['model'=16,'data'=8] {'model'}, use_global_device_ids=true, to_apply=%region_12.13 | all-reduce | flops 1 | bytes 8 | tf_op jit(solution)/shard_map/psum | solution.py:51
  1336.1 29.9 %all-reduce.12.cloned.1.call-done = (f32[2048,128]{1,0:T(8,128)}, f32[128,2048]{1,0:T(8,128)}, f32[2048,128]{1,0:T(8,128)}) async-done(((f32[2048,128]{1,0:T(8,128)}, f32[128,2048]{1,0:T(8,128)}, f32[2048,128]{1,0:T(8,128)}), (f32[2048,128]{1,0:T(8,128)}, f32[128,2048]{1,0:T(8,128)}, f32[2048,128]{1,0:T(8,128)})) %all-reduce.12.cloned.1.call-update) | async-done | bytes 3145744 | tf_op jit(solution)/shard_map/psum | solution.py:67
  1366.0 2.3 copy.31
  1368.3 2.3 copy.32
  1370.6 2.3 copy.33
  (49 shorter events, 0.4 us)
Async XLA Ops:
  7.2 463.4 %copy-start = (bf16[2048,128]{1,0:T(8,128)(2,1)S(1)}, bf16[2048,128]{1,0:T(8,128)(2,1)}, u32[]{:S(2)}) copy-start(bf16[2048,128]{1,0:T(8,128)(2,1)} %param.14) | copy-start | bytes 1572868
  7.2 427.8 %all-reduce.6.cloned.1.call-start = ((), (), s32[]{:S(2)}) async-start(), calls=%async_computation.1 | async-start | bytes 67108864 | tf_op jit(solution)/shard_map/psum | solution.py:36
  7.2 22.0 %copy-start.12 = (f32[128]{0:T(128)S(1)}, f32[128]{0:T(128)}, u32[]{:S(2)}) copy-start(f32[128]{0:T(128)} %param.15) | copy-start | bytes 1540
  7.2 22.5 %copy-start.8 = (bf16[128,2048]{1,0:T(8,128)(2,1)S(1)}, bf16[128,2048]{1,0:T(8,128)(2,1)}, u32[]{:S(2)}) copy-start(bf16[128,2048]{1,0:T(8,128)(2,1)} %param.13) | copy-start | bytes 1572868
  7.3 22.5 %copy-start.13 = (f32[128]{0:T(128)S(1)}, f32[128]{0:T(128)}, u32[]{:S(2)}) copy-start(f32[128]{0:T(128)} %param.16) | copy-start | bytes 1540
  16.0 26.8 %copy-start.3 = (f32[2,2048,128]{2,1,0:T(8,128)}, f32[2,2048,128]{2,1,0:T(8,128)S(1)}, u32[]{:S(2)}) copy-start(f32[2,2048,128]{2,1,0:T(8,128)S(1)} %get-tuple-element.37) | copy-start | bytes 6291460
  42.9 427.7 %copy-start.10 = (f32[2048]{0:T(1024)S(1)}, f32[2048]{0:T(1024)}, u32[]{:S(2)}) copy-start(f32[2048]{0:T(1024)} %param.17) | copy-start | bytes 24580
  42.9 427.7 %copy-start.11 = (f32[2048]{0:T(1024)S(1)}, f32[2048]{0:T(1024)}, u32[]{:S(2)}) copy-start(f32[2048]{0:T(1024)} %param.18) | copy-start | bytes 24580
  42.9 531.9 %all-gather.3.cloned.1.call-start = ((), (), s32[]{:S(2)}) async-start(), calls=%async_computation.5 | async-start | bytes 8912896 | tf_op jit(solution)/shard_map/all_gather | solution.py:43
  500.2 1.0 copy-start.7
  502.0 139.8 %all-reduce.8.cloned.1.call-start = ((), (), s32[]{:S(2)}) async-start(), calls=%async_computation.2 | async-start | bytes 2097152 | tf_op jit(solution)/shard_map/psum | solution.py:45
  580.6 182.2 %reduce-scatter.2.cloned.1.call-start = ((), (), s32[]{:S(2)}) async-start(), calls=%async_computation.3 | async-start | bytes 17825792 | tf_op jit(solution)/shard_map/reduce_scatter | solution.py:55
  651.3 531.7 %all-reduce.10.cloned.1.call-start = ((), (), s32[]{:S(2)}) async-start(), calls=%async_computation.4 | async-start | bytes 67108864 | tf_op jit(solution)/shard_map/psum | solution.py:62
  780.3 1.0 copy-start.5
  794.4 1.2 copy-start.6
  794.4 571.6 %all-reduce.12.cloned.1.call-start = ((), (), s32[]{:S(2)}) async-start(), calls=%async_computation.6 | async-start | bytes 6291456 | tf_op jit(solution)/shard_map/psum | solution.py:67
  1228.6 29.1 %copy-start.4 = (f32[2,2048,128]{2,1,0:T(8,128)S(1)}, f32[2,2048,128]{2,1,0:T(8,128)}, u32[]{:S(2)}) copy-start(f32[2,2048,128]{2,1,0:T(8,128)} %copy-done.3) | copy-start | bytes 6291460
  1257.7 10.9 copy-start.2
  1257.7 11.0 copy-start.9
  1268.7 22.2 %copy-start.14 = (f32[2,128]{1,0:T(2,128)S(1)}, f32[2,128]{1,0:T(2,128)}, u32[]{:S(2)}) copy-start(f32[2,128]{1,0:T(2,128)} %get-tuple-element.33) | copy-start | bytes 3076
  1290.9 81.9 %copy-start.1 = (bf16[2048,128]{1,0:T(8,128)(2,1)S(1)}, bf16[2048,128]{1,0:T(8,128)(2,1)}, u32[]{:S(2)}) copy-start(bf16[2048,128]{1,0:T(8,128)(2,1)} %param.14) | copy-start | bytes 1572868
Sparse Core Ops, SparseCore 0:
  43.0 391.9 all-reduce.5
  502.1 72.5 all-gather.2
  580.7 60.9 all-reduce.7
  651.4 111.3 reduce-scatter.1
  794.5 388.4 all-reduce.9
  1301.1 64.8 all-reduce.11
where the time goes:
time: 1390 us; the launch traced here: 1380 us
  waiting for transfers between devices  1030 us (74%)
  blocking collectives  136 us (10%)
  matrix products  111 us (8%)
  other arithmetic  72.2 us (5%)
  between operations  15.2 us (1%)
    psum x1, waiting for transfers between devices, shard_body(): lax.psum(jnp.einsum('woe,ef->wof', act_one, w_two, preferred_element_type...  392 us
    psum x1, waiting for transfers between devices, shard_body(): lax.psum(jnp.einsum('wof,ef->woe', d_out, w_three, preferred_element_type...  373 us
    reduce_scatter x1, waiting for transfers between devices, shard_body(): lax.psum_scatter(d_part_b, 'model', scatter_dimension=1, tiled=True)  104 us
    all_gather x1, waiting for transfers between devices, shard_body(): emb_b_full = lax.all_gather(embed_bf[1], 'model', axis=1, tiled=True)  72.7 us
    psum x1, waiting for transfers between devices, shard_body(): corr_mat = lax.psum(corr_part, 'data') / total_rows  60 us
    psum x3, blocking collectives, batch_norm(): moments = lax.psum(local_sums, 'data') / total_rows  51.2 us
    psum x2, blocking collectives, bn_backward(): global_sums = lax.psum(local_sums, 'data')  38.5 us
    psum x1, blocking collectives, shard_body(): loss_val = lax.psum(loss_part, 'model')  33 us
  transfers between devices with their start and end apart: 6, of which 6 were waited for; matrix products, arithmetic and copies ran while one was open for 2% of the time, Pallas kernels for 0%

commit v1 on v0

v1 whole, which is shorter than its diff:
```python
import jax
import jax.numpy as jnp
from jax import lax
from jax.sharding import PartitionSpec as P

BN_EPS = 1e-5
ALL = ('model', 'data')


def batch_norm(pre_act, total_rows):
    local_sums = jnp.stack([jnp.sum(pre_act, axis=1, keepdims=True), jnp.sum(pre_act * pre_act, axis=1, keepdims=True)])
    moments = lax.psum(local_sums, ALL) / total_rows
    inv_std = lax.rsqrt(moments[1] - moments[0] * moments[0] + BN_EPS)
    return (pre_act - moments[0]) * inv_std, inv_std


def bn_backward(d_act, lin_val, norm_val, inv_std, gamma_vec, total_rows):
    d_lin = jnp.where(lin_val > 0, d_act, 0.0)
    local_sums = jnp.stack([jnp.sum(d_lin, axis=1, keepdims=True), jnp.sum(d_lin * norm_val, axis=1, keepdims=True)])
    global_sums = lax.psum(local_sums, ALL)
    d_pre = gamma_vec * inv_std * (d_lin - (global_sums[0] + norm_val * global_sums[1]) / total_rows)
    return d_pre.astype(jnp.bfloat16), jnp.sum(global_sums[1], axis=(0, 1)), jnp.sum(global_sums[0], axis=(0, 1))


def solution(mesh):
    data_size = mesh.shape['data']
    model_size = mesh.shape['model']

    def shard_body(h_a, h_b, w_one, w_two, w_three, g_one, b_one, g_two, b_two, lam_off):
        group_rows = h_a.shape[0]
        total_rows = group_rows * data_size
        rows = group_rows // model_size
        full_dim, feat_dev = w_three.shape
        mid = lax.axis_index('model')
        h_all = jnp.stack([h_a, h_b])
        h_loc = lax.dynamic_slice_in_dim(h_all, mid * rows, rows, axis=1)
        w1 = lax.all_gather(w_one, 'model', axis=1, tiled=True)
        w2 = lax.all_gather(w_two, 'model', axis=0, tiled=True)
        w3 = lax.all_gather(w_three, 'model', axis=1, tiled=True)
        gb = lax.all_gather(jnp.stack([g_one, b_one]), 'model', axis=1, tiled=True)
        g1, b1 = gb[0], gb[1]

        def mm(spec, a, b):
            return jnp.einsum(spec, a, b, preferred_element_type=jnp.float32)

        pre_one = mm('vnf,fd->vnd', h_loc, w1)
        norm_one, inv_one = batch_norm(pre_one, total_rows)
        lin_one = g1 * norm_one + b1
        act_one = jnp.maximum(lin_one, 0.0).astype(jnp.bfloat16)
        pre_two = mm('woe,ef->wof', act_one, w2)
        norm_two, inv_two = batch_norm(pre_two, total_rows)
        lin_two = g_two * norm_two + b_two
        act_two = jnp.maximum(lin_two, 0.0).astype(jnp.bfloat16)
        pre_out = mm('woe,ef->wof', act_two, w3)
        norm_out, inv_out = batch_norm(pre_out, total_rows)
        emb = norm_out.astype(jnp.bfloat16)
        corr = lax.psum_scatter(mm('ni,nj->ij', emb[0], emb[1]), ALL, scatter_dimension=0, tiled=True) / total_rows
        piece = corr.shape[0]
        did = mid * data_size + lax.axis_index('data')
        row_ids = did * piece + lax.broadcasted_iota(jnp.int32, (piece, 1), 0)
        is_diag = row_ids == lax.broadcasted_iota(jnp.int32, (1, full_dim), 1)
        lam = lam_off[0]
        loss = lax.psum(jnp.sum(jnp.where(is_diag, (1.0 - corr) * (1.0 - corr), lam * corr * corr)), ALL)
        grad_piece = jnp.where(is_diag, -2.0 * (1.0 - corr), 2.0 * lam * corr).astype(jnp.bfloat16)
        grad_c = lax.all_gather(grad_piece, ALL, axis=0, tiled=True)
        d_emb = jnp.stack([mm('nj,ij->ni', emb[1], grad_c), mm('ni,ij->nj', emb[0], grad_c)]) / total_rows
        emb_f = emb.astype(jnp.float32)
        sums = jnp.stack([jnp.sum(d_emb, axis=1, keepdims=True), jnp.sum(d_emb * emb_f, axis=1, keepdims=True)])
        gm = lax.psum(sums, ALL) / total_rows
        d_out = (inv_out * (d_emb - gm[0] - emb_f * gm[1])).astype(jnp.bfloat16)
        dw3 = lax.psum_scatter(mm('woe,wof->ef', act_two, d_out), 'model', scatter_dimension=1, tiled=True)
        d_act_two = mm('wof,ef->woe', d_out, w3)
        d_pre_two, dg_two, db_two = bn_backward(d_act_two, lin_two, norm_two, inv_two, g_two, total_rows)
        dw2 = lax.psum_scatter(mm('woe,wof->ef', act_one, d_pre_two), 'model', scatter_dimension=0, tiled=True)
        d_act_one = mm('wof,ef->woe', d_pre_two, w2)
        d_pre_one, dg_one, db_one = bn_backward(d_act_one, lin_one, norm_one, inv_one, g1, total_rows)
        d_cols = lax.all_to_all(d_pre_one, 'model', split_axis=2, concat_axis=1, tiled=True)
        dw1 = mm('vnf,vnd->fd', h_all, d_cols)
        dw1, dw2, dw3 = lax.psum((dw1, dw2, dw3), 'data')
        dgb = lax.dynamic_slice_in_dim(jnp.stack([dg_one, db_one]), mid * feat_dev, feat_dev, axis=1)
        return loss.reshape(1), dw1, dw2, dw3, dgb[0], dgb[1], dg_two, db_two

    in_specs = (P('data', None), P('data', None), P(None, 'model'), P('model', None), P(None, 'model'),
                P('model'), P('model'), P(), P(), P())
    out_specs = (P(), P(None, 'model'), P('model', None), P(None, 'model'), P('model'), P('model'), P(), P())
    return jax.shard_map(shard_body, mesh=mesh, in_specs=in_specs, out_specs=out_specs, check_vma=False)
```

time: 1390 us -> 1460 us (1.050)
  blocking collectives: 136 us -> 446 us
  waiting for transfers between devices: 1030 us -> 897 us
  other arithmetic: 72.2 us -> 12 us
  matrix products: 111 us -> 75.8 us
    psum x4 -> x1, waiting for transfers between devices: 855 us -> 69.7 us  [shard_body(): dw1, dw2, dw3 = lax.psum((dw1, dw2, dw3), 'data')]
    reduce_scatter x1 -> x3, waiting for transfers between devices: 104 us -> 692 us  [the longest x1 661 us: shard_body(): lax.psum_scatter(mm('ni,nj->ij', emb[0], emb[1]), ALL, scatter_dimension=...]
    psum x7 -> x6, blocking collectives: 136 us -> 394 us  [the longest x3 200 us: batch_norm(): moments = lax.psum(local_sums, ALL) / total_rows]
    all_gather x1 -> x4, waiting for transfers between devices: 72.7 us -> 134 us  [the longest x1 71.6 us: shard_body(): grad_c = lax.all_gather(grad_piece, ALL, axis=0, tiled=True)]
    reduce_sum x3 -> x0, other arithmetic: 36.9 us -> none  [the longest x1 22 us: bn_backward(): jnp.sum(d_lin, axis=1, keepdims=True)]
    dot_general x11, matrix products: 111 us -> 75.8 us  [mm(): return jnp.einsum(spec, a, b, preferred_element_type=jnp.float32)]
    all_to_all x0 -> x1, blocking collectives: none -> 31.7 us  [shard_body(): lax.all_to_all(d_pre_one, 'model', split_axis=2, concat_axis=1, tiled=True)]
    convert_element_type x1 -> x2, other arithmetic: 29.1 us -> 5.01 us  [bn_backward(): d_pre.astype(jnp.bfloat16)]
  transfers between devices with their start and end apart: 6 -> 8, of which waited for: 6 -> 7; matrix products, arithmetic and copies ran while one was open for 2% -> 4% of each run, Pallas kernels for 0% -> 0%
where the time goes in v1:
time: 1460 us
  waiting for transfers between devices  897 us (61%)
  blocking collectives  446 us (31%)
  matrix products  75.8 us (5%)
  between operations  15.1 us (1%)
    reduce_scatter x1, waiting for transfers between devices, shard_body(): lax.psum_scatter(mm('ni,nj->ij', emb[0], emb[1]), ALL, scatter_dimension=...  661 us
    psum x3, blocking collectives, batch_norm(): moments = lax.psum(local_sums, ALL) / total_rows  200 us
    dot_general x11, matrix products, mm(): return jnp.einsum(spec, a, b, preferred_element_type=jnp.float32)  75.8 us
    all_gather x1, waiting for transfers between devices, shard_body(): grad_c = lax.all_gather(grad_piece, ALL, axis=0, tiled=True)  71.6 us
    psum x1, waiting for transfers between devices, shard_body(): dw1, dw2, dw3 = lax.psum((dw1, dw2, dw3), 'data')  69.7 us
    psum x1, blocking collectives, bn_backward(): global_sums = lax.psum(local_sums, ALL)  65.9 us
    psum x1, blocking collectives, shard_body(): lax.psum(jnp.sum(jnp.where(is_diag, (1.0 - corr) * (1.0 - corr), lam * co...  65.1 us
    psum x1, blocking collectives, shard_body(): gm = lax.psum(sums, ALL) / total_rows  63 us
  transfers between devices with their start and end apart: 8, of which 7 were waited for; matrix products, arithmetic and copies ran while one was open for 4% of the time, Pallas kernels for 0%

profile of v1, /device:TPU:1, one launch (start us, length us, event | category | flops | bytes accessed | tf_op | source)
XLA Modules:
  0.0 1455.4 jit_solution(513155499322757460)
XLA Ops:
  7.2 0.7 all-gather.5.cloned.1.call-update
  7.9 0.7 all-gather.7.cloned.1.call-update
  8.7 0.7 all-gather.9.cloned.1.call-update
  9.4 0.7 pad_maximum_fusion.10
  10.1 20.8 %all_gather.15 = f32[2,2048]{1,0:T(2,128)S(1)} all-gather(f32[2,128]{1,0:T(2,128)S(1)} %pad_maximum_fusion.10), channel_id=1, replica_groups=mesh['model'=16,'data'=8] {'model'}, dimensions={1}, use_global_device_ids=true | all-gather | bytes 17408 | tf_op jit(solution)/shard_map/all_gather | solution.py:40
  30.9 57.5 %all-gather.5.cloned.1.call-done = bf16[2048,2048]{1,0:T(8,128)(2,1)} async-done(((bf16[2048,128]{1,0:T(8,128)(2,1)}), bf16[2048,2048]{1,0:T(8,128)(2,1)}) %all-gather.5.cloned.1.call-update) | async-done | bytes 8388624 | tf_op jit(solution)/shard_map/all_gather | solution.py:37
  88.5 6.1 fusion.45
  94.7 67.5 %psum.70 = f32[2,2,1,2048]{3,1,2,0:T(2,128)S(1)} all-reduce(f32[2,2,1,2048]{3,1,2,0:T(2,128)S(1)} %pad_maximum_fusion.4), channel_id=1, replica_groups=mesh['model'=16,'data'=8] {'model','data'}, use_global_device_ids=true, to_apply=%region_2.0 | all-reduce | flops 8192 | bytes 65536 | tf_op jit(solution)/shard_map/psum | solution.py:12
  162.2 0.7 all-gather.7.cloned.1.call-done
  163.0 7.1 fusion.44
  170.1 66.5 %psum.71 = f32[2,2,1,2048]{3,1,2,0:T(2,128)S(1)} all-reduce(f32[2,2,1,2048]{3,1,2,0:T(2,128)S(1)} %pad_maximum_fusion.5), channel_id=1, replica_groups=mesh['model'=16,'data'=8] {'model','data'}, use_global_device_ids=true, to_apply=%region_5.0 | all-reduce | flops 8192 | bytes 65536 | tf_op jit(solution)/shard_map/psum | solution.py:12
  236.7 4.2 all-gather.9.cloned.1.call-done
  240.8 6.4 fusion.43
  247.3 65.8 %psum.72 = f32[2,2,1,2048]{3,1,2,0:T(2,128)S(1)} all-reduce(f32[2,2,1,2048]{3,1,2,0:T(2,128)S(1)} %pad_maximum_fusion.6), channel_id=1, replica_groups=mesh['model'=16,'data'=8] {'model','data'}, use_global_device_ids=true, to_apply=%region_8.0 | all-reduce | flops 8192 | bytes 65536 | tf_op jit(solution)/shard_map/psum | solution.py:12
  313.1 0.2 multiply_convert_fusion.2
  313.3 8.1 fusion.25
  321.4 0.0 all-gather.11.cloned.1.call-start
  322.2 661.1 %reduce-scatter.4.cloned.1.call-done = f32[16,2048]{1,0:T(8,128)} async-done(((f32[2048,2048]{1,0:T(8,128)}), f32[16,2048]{1,0:T(8,128)}) %reduce-scatter.4.cloned.1.call-update) | async-done | bytes 131088 | tf_op jit(solution)/shard_map/reduce_scatter | solution.py:57
  983.3 2.2 select_convert_fusion
  985.6 71.6 %all-gather.11.cloned.1.call-done = bf16[2048,2048]{1,0:T(8,128)(2,1)} async-done(((bf16[16,2048]{1,0:T(8,128)(2,1)}), bf16[2048,2048]{1,0:T(8,128)(2,1)}) %all-gather.11.cloned.1.call-update) | async-done | bytes 8388624 | tf_op jit(solution)/shard_map/all_gather | solution.py:65
  1057.2 6.4 convolution_bitcast_fusion.3
  1063.7 1.3 convolution_bitcast_fusion.2
  1065.0 0.6 fusion.22
  1065.6 0.4 copy-done.4
  1066.0 63.0 %psum.74 = f32[2,2,1,2048]{3,1,2,0:T(2,128)S(1)} all-reduce(f32[2,2,1,2048]{3,1,2,0:T(2,128)S(1)} %pad_maximum_fusion.7), channel_id=1, replica_groups=mesh['model'=16,'data'=8] {'model','data'}, use_global_device_ids=true, to_apply=%region_14.15 | all-reduce | flops 8192 | bytes 65536 | tf_op jit(solution)/shard_map/psum | solution.py:69
  1129.0 2.2 fusion.21
  1131.3 8.1 convolution_bitcast_fusion
  1139.4 0.3 reduce-scatter.6.cloned.1.call-start
  1139.7 1.3 copy-done.6
  1141.0 7.5 fusion.42
  1148.6 65.9 %psum.75 = f32[2,2,1,2048]{3,1,2,0:T(2,128)S(1)} all-reduce(f32[2,2,1,2048]{3,1,2,0:T(2,128)S(1)} %pad_maximum_fusion.8), channel_id=1, replica_groups=mesh['model'=16,'data'=8] {'model','data'}, use_global_device_ids=true, to_apply=%region_17.18 | all-reduce | flops 8192 | bytes 65536 | tf_op jit(solution)/shard_map/psum | solution.py:20
  1214.5 0.6 slice_reduce_fusion.3
  1215.1 2.9 multiply_convert_fusion.1
  1218.0 8.1 convolution_bitcast_fusion.1
  1226.2 7.5 fusion.41
  1233.7 65.1 %all-reduce = (f32[1]{0:T(128)}, f32[2,2,1,2048]{3,1,2,0:T(2,128)S(1)}) all-reduce(f32[1]{0:T(128)} %bitcast.24, f32[2,2,1,2048]{3,1,2,0:T(2,128)S(1)} %pad_maximum_fusion.9), channel_id=1, replica_groups=mesh['model'=16,'data'=8] {'model','data'}, use_global_device_ids=true, to_apply=%region_11.12 | all-reduce | flops 8193 | bytes 65544 | tf_op jit(solution)/shard_map/psum | solution.py:63
  1298.9 2.1 multiply_convert_fusion
  1301.0 0.8 copy.22
  1301.8 31.7 %all_to_all.18 = bf16[2,128,2048]{1,0,2:T(2,128)(2,1)S(1)} all-to-all(bf16[2,128,2048]{1,0,2:T(2,128)(2,1)S(1)} %copy.22), channel_id=1, replica_groups=mesh['model'=16,'data'=8] {'model'}, dimensions={2} | all-to-all | bytes 2097152 | tf_op jit(solution)/shard_map/all_to_all | solution.py:77
  1333.5 0.9 copy.23
  1334.4 9.1 fusion.17
  1343.5 30.4 %reduce-scatter.6.cloned.1.call-done = f32[128,2048]{1,0:T(8,128)} async-done(((f32[2048,2048]{1,0:T(8,128)}), f32[128,2048]{1,0:T(8,128)}) %reduce-scatter.6.cloned.1.call-update) | async-done | bytes 1048592 | tf_op jit(solution)/shard_map/reduce_scatter | solution.py:74
  1373.9 0.1 fusion.37
  1374.0 0.5 slice_bitcast_fusion.18
  1374.5 69.7 %all-reduce.4.cloned.1.call-done = (f32[2048,128]{1,0:T(8,128)}, f32[128,2048]{1,0:T(8,128)}, f32[2048,128]{1,0:T(8,128)}) async-done(((f32[2048,128]{1,0:T(8,128)}, f32[128,2048]{1,0:T(8,128)}, f32[2048,128]{1,0:T(8,128)}), (f32[2048,128]{1,0:T(8,128)}, f32[128,2048]{1,0:T(8,128)}, f32[2048,128]{1,0:T(8,128)})) %all-reduce.4.cloned.1.call-update) | async-done | bytes 3145744 | tf_op jit(solution)/shard_map/psum | solution.py:79
  1444.3 2.4 copy.34
  1446.7 1.0 copy.35
  1447.6 1.0 copy.36
  (52 shorter events, 0.7 us)
Async XLA Ops:
  7.2 81.3 %all-gather.5.cloned.1.call-start = ((), (), s32[]{:S(2)}) async-start(), calls=%async_computation.4 | async-start | bytes 8912896 | tf_op jit(solution)/shard_map/all_gather | solution.py:37
  7.9 155.1 %all-gather.7.cloned.1.call-start = ((), (), s32[]{:S(2)}) async-start(), calls=%async_computation.5 | async-start | bytes 8912896 | tf_op jit(solution)/shard_map/all_gather | solution.py:38
  8.7 232.2 %all-gather.9.cloned.1.call-start = ((), (), s32[]{:S(2)}) async-start(), calls=%async_computation.6 | async-start | bytes 8912896 | tf_op jit(solution)/shard_map/all_gather | solution.py:39
  9.4 973.9 %reduce-scatter.4.cloned.1.call-start = ((), (), s32[]{:S(2)}) async-start(), calls=%async_computation.7 | async-start | bytes 16908288 | tf_op jit(solution)/shard_map/reduce_scatter | solution.py:57
  94.6 75.4 %copy-start.1 = (f32[2,128,2048]{2,1,0:T(8,128)}, f32[2,128,2048]{2,1,0:T(8,128)S(1)}, u32[]{:S(2)}) copy-start(f32[2,128,2048]{2,1,0:T(8,128)S(1)} %get-tuple-element.45) | copy-start | bytes 6291460
  163.0 73.7 %copy-start.9 = (f32[2048]{0:T(1024)S(1)}, f32[2048]{0:T(1024)}, u32[]{:S(2)}) copy-start(f32[2048]{0:T(1024)} %param.17) | copy-start | bytes 24580
  163.0 77.8 %copy-start.10 = (f32[2048]{0:T(1024)S(1)}, f32[2048]{0:T(1024)}, u32[]{:S(2)}) copy-start(f32[2048]{0:T(1024)} %param.18) | copy-start | bytes 24580
  321.4 735.8 %all-gather.11.cloned.1.call-start = ((), (), s32[]{:S(2)}) async-start(), calls=%async_computation.8 | async-start | bytes 8454144 | tf_op jit(solution)/shard_map/all_gather | solution.py:65
  985.6 357.9 %reduce-scatter.8.cloned.1.call-start = ((), (), s32[]{:S(2)}) async-start(), calls=%async_computation.10 | async-start | bytes 17825792 | tf_op jit(solution)/shard_map/reduce_scatter | solution.py:71
  1057.2 6.4 copy-start
  1063.7 1.3 copy-start.3
  1065.0 1.0 copy-start.4
  1129.0 2.2 copy-start.5
  1139.4 1.6 copy-start.6
  1139.4 234.4 %reduce-scatter.6.cloned.1.call-start = ((), (), s32[]{:S(2)}) async-start(), calls=%async_computation.9 | async-start | bytes 17825792 | tf_op jit(solution)/shard_map/reduce_scatter | solution.py:74
  1215.1 2.9 copy-start.2
  1226.2 218.1 %all-reduce.4.cloned.1.call-start = ((), (), s32[]{:S(2)}) async-start(), calls=%async_computation.11 | async-start | bytes 6291456 | tf_op jit(solution)/shard_map/psum | solution.py:79
  1444.2 2.4 copy-start.8
  1444.2 3.4 copy-start.7
Sparse Core Ops, SparseCore 0:
  10.1 78.3 all-gather.4
  90.6 72.2 all-gather.6
  165.1 75.6 all-gather.8
  321.6 661.6 reduce-scatter.3
  986.7 70.4 all-gather.10
  1139.6 108.7 reduce-scatter.7
  1251.8 122.0 reduce-scatter.5
  1377.0 67.1 all-reduce.3

commit v2 on v0

v2 whole, which is shorter than its diff:
```python
import functools

import jax
import jax.numpy as jnp
from jax import lax
from jax.experimental import pallas as pl
from jax.experimental.pallas import tpu as pltpu
from jax.sharding import PartitionSpec as P

BN_EPS = 1e-5
MESH_ID = pl.DeviceIdType.MESH
RING = 4
PAIR = 2
AXES = ('z', 'y', 'x')
ORDERS = (('x', 'y', 'z'), ('y', 'z', 'x'), ('z', 'x', 'y'))
LANES = tuple((sub, colour) for sub in range(PAIR) for colour in range(3))
OTHERS = (1, 2, 3)
N_SEND = 250
N_RECV = 480
F32 = jnp.float32
BF16 = jnp.bfloat16
WHOLE = slice(None)


def dot_nn(a, b):
    return lax.dot_general(a, b, (((1,), (0,)), ((), ())), preferred_element_type=F32)


def dot_nt(a, b):
    return lax.dot_general(a, b, (((1,), (1,)), ((), ())), preferred_element_type=F32)


def dot_tn(a, b):
    return lax.dot_general(a, b, (((0,), (0,)), ((), ())), preferred_element_type=F32)


def col_sum(value):
    return jnp.sum(value, axis=0, keepdims=True)


def lanes_of(values):
    return jnp.concatenate(list(values), axis=1)


def wrap(value):
    return lax.rem(value, RING)


def step(*gens):
    for gen in gens:
        next(gen, None)


def finish(gens):
    live = list(gens)
    while live:
        live = [gen for gen in live if next(gen, WHOLE) is not WHOLE]


def mega_kernel(cfg, h_a, h_b, w_one, w_two, w_three, g_one, b_one, g_two, b_two, lam_ref,
                dw_out, small_out,
                hx, u1, u2, u3, xf1, xf2, zf, wg1, wq1, wg2, wq2, wg3, part, part2, rv1, rv2, rv3,
                gbuf, stat, sres, dgb, du1, a2a, out_w, ssem, rsem, lsem, hsem, credit):
    blk, rows, total_rows, splits = cfg
    half = 8 * blk
    quad = PAIR * blk
    vrows = PAIR * rows
    inv_n = 1.0 / total_rows

    mid = lax.axis_index('model')
    did = lax.axis_index('data')
    core = lax.rem(did, PAIR)
    other = 1 - core
    coord = {'z': lax.div(mid, RING), 'y': wrap(mid), 'x': lax.div(did, PAIR)}
    zc, yc, xc = coord['z'], coord['y'], coord['x']
    near = {axis: [coord[axis]] + [wrap(coord[axis] + off) for off in OTHERS] for axis in AXES}
    z_base, x_base = zc * RING, xc * PAIR
    targets_of = {'z': [(q * RING + yc, did) for q in near['z']], 'y': [(z_base + q, did) for q in near['y']],
                  'x': [(mid, q * PAIR + core) for q in near['x']]}
    peer = (mid, x_base + other)

    def device(axis, off):
        return targets_of[axis][off]

    z_own, z_other = PAIR * core, PAIR * other
    counters = {'s': 0, 'r': 0, 'l': 0}

    def new_ids(kind, count):
        first = counters[kind]
        counters[kind] = first + count
        assert counters[kind] <= {'s': N_SEND, 'r': N_RECV, 'l': 16}[kind]
        return list(range(first, first + count))

    def rcopy(src, dst, send_id, recv_id, target):
        return pltpu.make_async_remote_copy(src_ref=src, dst_ref=dst, send_sem=ssem.at[send_id],
                                            recv_sem=rsem.at[recv_id], device_id=target, device_id_type=MESH_ID)

    def band(sub, colour):
        begin = 0
        for size in splits[sub][:colour]:
            begin += size
        return pl.ds(begin, splits[sub][colour])

    def gather_lane(buf, sub, colour, sid, rid):
        order = ORDERS[colour]
        rsl = band(sub, colour)

        def region(axis, have, q, part_id=None):
            idx = dict(coord)
            idx[axis] = q
            for name in have:
                idx[name] = pl.ds(0, RING)
            if part_id is not None:
                idx[have[-1]] = pl.ds(PAIR * part_id, PAIR)
            return buf.at[idx['z'], idx['y'], idx['x'], sub, rsl, :]

        axis = order[0]
        own = region(axis, (), coord[axis])
        pending = [rcopy(own, own, sid[off - 1], rid[off - 1], device(axis, off)) for off in OTHERS]
        for copy in pending:
            copy.start()
        yield
        for copy in pending:
            copy.wait_recv()
        for phase in (1, 2):
            axis, have = order[phase], order[:phase]
            base = phase * RING - 1
            p = coord[axis]
            up, down = device(axis, 1), device(axis, 3)
            own = region(axis, have, p)
            to_up = rcopy(own, own, sid[base], rid[base], up)
            to_down = rcopy(own, own, sid[base + 1], rid[base + 1], down)
            to_up.start()
            to_down.start()
            yield
            to_up.wait_recv()
            src = region(axis, have, near[axis][3], 0)
            relay_up = rcopy(src, src, sid[base + 2], rid[base + 2], up)
            relay_up.start()
            to_down.wait_recv()
            src = region(axis, have, near[axis][1], 1)
            relay_down = rcopy(src, src, sid[base + 3], rid[base + 3], down)
            relay_down.start()
            yield
            relay_up.wait_recv()
            relay_down.wait_recv()
            pending.extend((to_up, to_down, relay_up, relay_down))
        for copy in pending:
            copy.wait_send()

    def gather_lanes(buf, send_ids, recv_ids):
        width = 11
        return [gather_lane(buf, sub, colour, send_ids[k * width:(k + 1) * width], recv_ids[k * width:(k + 1) * width])
                for k, (sub, colour) in enumerate(LANES)]

    def scatter_lane(buf, bank, sub, colour, sid, rid, give, take):
        order = ORDERS[colour]
        rsl = band(sub, colour)
        pending = []
        for phase in (0, 1):
            axis = order[phase]
            left = tuple(name for name in AXES if name in order[phase + 1:])
            p = coord[axis]
            base = phase * 6

            def region(q, part_id, axis=axis, left=left):
                idx = dict(coord)
                idx[axis] = q
                for name in left[:-1]:
                    idx[name] = pl.ds(0, RING)
                idx[left[-1]] = pl.ds(PAIR * part_id, PAIR)
                return buf.at[idx['z'], idx['y'], idx['x'], sub, rsl, :]

            def landing(slot, phase=phase):
                if phase:
                    return rv2.at[bank, sub, slot, :, rsl, :]
                return rv1.at[sub, slot, :, :, rsl, :]

            def add(q, part_id, slots, axis=axis, left=left, phase=phase):
                def one(i, j):
                    idx = dict(coord)
                    idx[axis] = q
                    idx[left[-1]] = PAIR * part_id + j
                    if not phase:
                        idx[left[0]] = i
                    total = buf[idx['z'], idx['y'], idx['x'], sub, rsl, :]
                    for slot in slots:
                        total = total + (rv2[bank, sub, slot, j, rsl, :] if phase else rv1[sub, slot, i, j, rsl, :])
                    buf[idx['z'], idx['y'], idx['x'], sub, rsl, :] = total

                if phase:
                    for j in range(PAIR):
                        one(0, j)
                else:
                    @pl.loop(0, RING)
                    def _(i):
                        for j in range(PAIR):
                            one(i, j)

            up, down = device(axis, 1), device(axis, 3)
            p1, p2, p3 = near[axis][1:]
            if take is not None and not phase:
                pl.semaphore_wait(credit.at[take], PAIR)
            relay_up = rcopy(region(p2, 1), landing(0), sid[base], rid[base], up)
            relay_down = rcopy(region(p2, 0), landing(1), sid[base + 1], rid[base + 1], down)
            own_up = rcopy(region(p1, 0), landing(2), sid[base + 2], rid[base + 2], up)
            own_down = rcopy(region(p3, 1), landing(3), sid[base + 3], rid[base + 3], down)
            relay_up.start()
            relay_down.start()
            if not phase:
                yield
            own_up.start()
            own_down.start()
            yield
            relay_up.wait_recv()
            add(p1, 1, (0,))
            sum_up = rcopy(region(p1, 1), landing(4), sid[base + 4], rid[base + 4], up)
            sum_up.start()
            relay_down.wait_recv()
            add(p3, 0, (1,))
            sum_down = rcopy(region(p3, 0), landing(5), sid[base + 5], rid[base + 5], down)
            sum_down.start()
            yield
            own_up.wait_recv()
            sum_down.wait_recv()
            add(p, 0, (2, 5))
            own_down.wait_recv()
            sum_up.wait_recv()
            add(p, 1, (3, 4))
            if give is not None and not phase:
                for target in (up, down):
                    pl.semaphore_signal(credit.at[give], inc=1, device_id=target, device_id_type=MESH_ID)
            pending.extend((relay_up, relay_down, own_up, own_down, sum_up, sum_down))
        axis = order[2]
        p = coord[axis]
        base = 12
        last = []
        for k, off in enumerate(OTHERS):
            idx = dict(coord)
            idx[axis] = near[axis][off]
            last.append(rcopy(buf.at[idx['z'], idx['y'], idx['x'], sub, rsl, :], rv3.at[bank, sub, k, rsl, :],
                              sid[base + k], rid[base + k], device(axis, off)))
        for copy in last:
            copy.start()
        yield
        for copy in last:
            copy.wait_recv()
        got = [rv3[bank, sub, k, rsl, :] for k in range(3)]
        buf[zc, yc, xc, sub, rsl, :] = (buf[zc, yc, xc, sub, rsl, :] + got[0]) + (got[1] + got[2])
        for copy in pending + last:
            copy.wait_send()

    def scatter_lanes(buf, bank, send_ids, recv_ids, give=None, take=None):
        width = 15
        return [scatter_lane(buf, bank, sub, colour, send_ids[k * width:(k + 1) * width],
                             recv_ids[k * width:(k + 1) * width], k if give else None, k if take else None)
                for k, (sub, colour) in enumerate(LANES)]

    def quarter(src, dst, sub, send_id, recv_id):
        copy = rcopy(src.at[pl.ds(z_other, PAIR), :, :, sub], dst.at[:, :, :, sub], send_id, recv_id, peer)
        copy.start()
        return copy

    stat_recv = [new_ids('r', 9) for _ in range(PAIR)]
    stat_send = new_ids('s', 9)

    def stat_sum(parity, width, fill=None):
        pending = []
        for d, axis in enumerate(AXES):
            own = stat.at[parity, d, coord[axis], :, pl.ds(0, width)]
            copies = [rcopy(own, own, stat_send[d * 3 + off - 1], stat_recv[parity][d * 3 + off - 1], device(axis, off))
                      for off in OTHERS]
            for copy in copies:
                copy.start()
            if fill is not None:
                step(*fill[d])
            for copy in copies:
                copy.wait_recv()
            got = [stat[parity, d, q, :, 0:width] for q in range(RING)]
            total = (got[0] + got[1]) + (got[2] + got[3])
            if axis != 'x':
                stat[parity, d + 1, coord[AXES[d + 1]], :, 0:width] = total
            pending.extend(copies)
        for copy in pending:
            copy.wait_send()
        return total

    def row(k):
        return slice(k, k + 1)

    def first_row(v):
        return row(PAIR * v)

    def second_row(v):
        return row(PAIR * v + 1)

    def put_stat(parity, v, cols, first, second):
        stat[parity, 0, zc, first_row(v), cols] = first
        stat[parity, 0, zc, second_row(v), cols] = second

    def local(src, dst):
        copy = pltpu.make_async_copy(src, dst, lsem.at[new_ids('l', 1)[0]])
        copy.start()
        return copy

    row0 = pl.multiple_of(core * half + xc * quad, quad)
    subs = range(PAIR)
    w1_loads = [local(w_one.at[pl.ds(row0 + s * blk, blk), :], wg1.at[zc, yc, xc, s]) for s in subs]
    hrow = pl.multiple_of(mid * rows, rows)
    h_ids = [new_ids('s', RING), new_ids('r', RING)]
    h_pairs = []
    for v, h_ref in enumerate((h_a, h_b)):
        for kh in subs:
            h_pairs.append((h_ref.at[pl.ds(hrow, rows), pl.ds(kh * half, half)],
                            hx.at[kh, pl.ds(pl.multiple_of(v * vrows + core * rows, rows), rows), :]))
    more_loads = [local(src, dst) for src, dst in h_pairs]
    more_loads.append(local(g_one, gbuf.at[zc, yc, row(0), :]))
    more_loads.append(local(b_one, gbuf.at[zc, yc, row(1), :]))
    for s in subs:
        more_loads.append(local(w_two.at[:, pl.ds(row0 + s * blk, blk)], wg2.at[zc, yc, xc, s]))
        more_loads.append(local(w_three.at[pl.ds(row0 + s * blk, blk), :], wg3.at[zc, yc, xc, s]))

    barrier = pltpu.get_barrier_semaphore()
    greeted = [device(axis, off) for axis in AXES for off in OTHERS] + [peer]
    for target in greeted:
        pl.semaphore_signal(barrier, inc=1, device_id=target, device_id_type=MESH_ID)
    pl.semaphore_wait(barrier, len(greeted))

    gather_width = 66
    send_a, send_b = new_ids('s', 90), new_ids('s', 90)
    gather_recv = [new_ids('r', gather_width) for _ in range(3)]
    scatter_recv = [new_ids('r', 90), gather_recv[1] + gather_recv[2][:24]]
    q_send, q_recv = new_ids('s', 8), new_ids('r', 8)

    for copy in w1_loads:
        copy.wait()
    lanes1 = gather_lanes(wg1, send_a, gather_recv[0])
    step(*lanes1)
    h_copies = [rcopy(src, dst, h_ids[0][k], h_ids[1][k], peer) for k, (src, dst) in enumerate(h_pairs)]
    for copy in h_copies:
        copy.start()
    for copy in more_loads:
        copy.wait()

    gb_recv = new_ids('r', 6)

    def gain_copies(k, axis, own):
        made = [rcopy(own, own, stat_send[k + off - 1], gb_recv[k + off - 1], device(axis, off)) for off in OTHERS]
        for copy in made:
            copy.start()
        return made

    gb_y = gain_copies(0, 'y', gbuf.at[zc, yc])
    lanes2 = gather_lanes(wg2, send_b, gather_recv[1])
    lanes3 = gather_lanes(wg3, send_a, gather_recv[2])
    step(*lanes1)
    for copy in gb_y:
        copy.wait_recv()
    gb_z = gain_copies(3, 'z', gbuf.at[zc])
    step(*lanes2)
    step(*lanes1)
    step(*lanes1)
    step(*lanes2)
    step(*lanes1)
    step(*lanes2)
    q1 = []
    for s in subs:
        finish(lanes1[s * 3:s * 3 + 3])
        q1.append(quarter(wg1, wq1, s, q_send[s], q_recv[s]))
    for copy in gb_z:
        copy.wait_recv()
    for copy in gb_y + gb_z:
        copy.wait_send()
    for copy in h_copies:
        copy.wait_recv()
    step(*lanes2[:3])
    for copy in q1:
        copy.wait_recv()

    def gathered(k):
        return lanes_of(gbuf[z, i, row(k), :] for z in (z_own, z_own + 1) for i in range(RING))

    gain1, shift1 = gathered(0), gathered(1)
    my_cols = pl.ds(pl.multiple_of(core * half, half), half)
    gain2, shift2 = g_two[:, my_cols], b_two[:, my_cols]
    for k, value in enumerate((gain1, shift1, gain2, shift2)):
        sres[3, row(k), :] = value

    def view_rows(v):
        return pl.ds(v * vrows, vrows)

    def chunk_cols(j):
        return pl.ds(pl.multiple_of(j * quad, quad), quad)

    def over_chunks(fn):
        pl.loop(0, RING)(fn)

    def forward_rowsplit(act, own, got, views, emit, ready):
        for v, src_v in views:
            ready[v]()

            def body(j):
                zz, y0 = lax.div(j, PAIR), lax.rem(j, PAIR) * PAIR
                sides = [lanes_of(ref[z, yy].reshape(half, blk) for yy in (y0, y0 + 1))
                         for ref, z in ((own, z_own + zz), (got, zz))]
                emit(j, v, dot_nn(act[core, view_rows(src_v), :], sides[0])
                     + dot_nn(act[other, view_rows(src_v), :], sides[1]))
            over_chunks(body)

    def forward_colsplit(act, own, emit, ready):
        for v in subs:
            ready[v]()

            def body(j):
                sides = [lanes_of(own[PAIR * hh:PAIR * hh + PAIR, :, j, s].reshape(half, blk) for s in subs)
                         for hh in subs]
                emit(j, v, dot_nn(act[0, view_rows(v), :], sides[0]) + dot_nn(act[1, view_rows(v), :], sides[1]))
            over_chunks(body)

    def backward_rowsplit(act, own, views, emit, ready):
        for v, src_v in views:
            ready[v]()

            def body(j):
                sides = [lanes_of(own[PAIR * hh + i // RING, i % RING, j].reshape(quad, blk) for i in range(8))
                         for hh in subs]
                emit(j, v, dot_nt(act[0, view_rows(src_v), :], sides[0])
                     + dot_nt(act[1, view_rows(src_v), :], sides[1]))
            over_chunks(body)

    def backward_colsplit(act, own, got, emit, ready):
        for v in subs:
            ready[v]()

            def body(j):
                sides = []
                zz, y0 = lax.div(j, PAIR), lax.rem(j, PAIR) * PAIR
                for ref, z in ((own, z_own + zz), (got, zz)):
                    bands = [lanes_of(ref[z, yy, t // PAIR, t % PAIR] for t in range(8)) for yy in (y0, y0 + 1)]
                    sides.append(jnp.concatenate(bands, axis=0))
                emit(j, v, dot_nt(act[core, view_rows(v), :], sides[0]) + dot_nt(act[other, view_rows(v), :], sides[1]))
            over_chunks(body)

    def partial_rowsplit(dst, lhs, lhs_rows, rhs, rhs_rows):
        def body(j):
            left = lhs[core, lhs_rows, chunk_cols(j)]
            for hh in subs:
                for t in range(RING):
                    res = dot_tn(left, rhs[hh, rhs_rows, t * quad:(t + 1) * quad])
                    for i in subs:
                        for s in subs:
                            dst[PAIR * hh + t // PAIR, (t % PAIR) * PAIR + i, j, s] = res[s * blk:(s + 1) * blk,
                                                                                         i * blk:(i + 1) * blk]
        over_chunks(body)

    def partial_colsplit(dst, lhs, rhs, hh):
        def body(t):
            left = lhs[hh, :, chunk_cols(t)]
            zz, y0 = PAIR * hh + lax.div(t, PAIR), lax.rem(t, PAIR) * PAIR
            for q in range(RING):
                res = dot_tn(left, rhs[core, :, q * quad:(q + 1) * quad])
                for i, yy in enumerate((y0, y0 + 1)):
                    for s in subs:
                        dst[zz, yy, q, s] = res[i * blk:(i + 1) * blk, s * blk:(s + 1) * blk]
        over_chunks(body)

    def forward_emit(dst, parity):
        def emit(j, v, acc):
            cols = chunk_cols(j)
            dst[view_rows(v), cols] = acc
            put_stat(parity, v, cols, col_sum(acc), col_sum(acc * acc))
        return emit

    def moments(total, slot):
        for v in subs:
            mean = total[first_row(v), 0:half] * inv_n
            inv = lax.rsqrt(total[second_row(v), 0:half] * inv_n - mean * mean + BN_EPS)
            sres[slot, first_row(v), :] = mean
            sres[slot, second_row(v), :] = inv

    act_send, act_recv = new_ids('s', PAIR), new_ids('r', 10)

    def share(dst, v):
        region = dst.at[core, view_rows(v), :]
        copy = rcopy(region, region, act_send[v], act_recv.pop(), peer)
        copy.start()
        return copy

    rstep = min(32, vrows)

    def apply_rows(v, fn):
        @pl.loop(0, vrows // rstep)
        def _(i):
            fn(pl.ds(pl.multiple_of(v * vrows + i * rstep, rstep), rstep))

    def activate(src, slot, gain, shift, dst):
        copies = []
        for v in subs:
            mean = sres[slot, first_row(v), :]
            inv = sres[slot, second_row(v), :]

            def fn(rsl, mean=mean, inv=inv):
                norm = (src[rsl, :] - mean) * inv
                if gain is not None:
                    norm = jnp.maximum(gain * norm + shift, 0.0)
                dst[core, rsl, :] = norm.astype(BF16)
            apply_rows(v, fn)
            copies.append(share(dst, v))
        return copies

    def received(copies):
        return [copy.wait_recv for copy in copies]

    def sent(copies):
        for copy in copies:
            copy.wait_send()

    def nothing():
        pass

    both = ((0, 0), (1, 1))
    at_once = (nothing, nothing)
    all_rows = pl.ds(0, PAIR * vrows)

    forward_rowsplit(hx, wg1, wq1, both, forward_emit(u1, 0), at_once)
    sub0, sub1 = lanes2[:3], lanes2[3:]
    moments(stat_sum(0, half, (sub0, (sub1[0], sub1[1]), (sub1[2],))), 0)
    copies = activate(u1, 0, gain1, shift1, xf1)
    sent(q1 + h_copies)
    finish(lanes2)
    q2 = [quarter(wg2, wq2, s, q_send[PAIR + s], q_recv[PAIR + s]) for s in subs]
    step(*lanes3)
    forward_colsplit(xf1, wg2, forward_emit(u2, 1), received(copies))
    sent(copies)
    step(*lanes3)
    sub0, sub1 = lanes3[:3], lanes3[3:]
    moments(stat_sum(1, half, (lanes3, sub0, (sub1[0], sub1[1]))), 1)
    copies = activate(u2, 1, gain2, shift2, xf2)
    step(sub1[2])
    q3 = []
    for s, group in enumerate((sub0, sub1)):
        finish(group)
        q3.append(quarter(wg3, wq1, s, q_send[RING + s], q_recv[RING + s]))
    for copy in q3:
        copy.wait_recv()
    forward_rowsplit(xf2, wg3, wq1, both, forward_emit(u3, 0), received(copies))
    sent(copies)
    moments(stat_sum(0, half), PAIR)
    copies = activate(u3, PAIR, None, None, zf)
    for copy in copies:
        copy.wait_recv()
    sent(copies)

    partial_rowsplit(part, zf, view_rows(0), zf, view_rows(1))
    lanes_c = scatter_lanes(part, 0, send_a, scatter_recv[0])
    lanes_g = gather_lanes(wg1, send_b, gather_recv[0])
    lam = lam_ref[0]
    col_ids = mid * blk + lax.broadcasted_iota(jnp.int32, (blk, blk), 1)

    def gradient_piece(s):
        corr = part[zc, yc, xc, s] * inv_n
        row_ids = core * half + xc * quad + s * blk + lax.broadcasted_iota(jnp.int32, (blk, blk), 0)
        diag = row_ids == col_ids
        terms = jnp.where(diag, (1.0 - corr) * (1.0 - corr), lam * corr * corr)
        wg1[zc, yc, xc, s] = jnp.where(diag, -2.0 * (1.0 - corr), 2.0 * lam * corr).astype(BF16)
        return jnp.sum(jnp.sum(terms, axis=0, keepdims=True), axis=1, keepdims=True)

    ca, cb = lanes_c[:3], lanes_c[3:]
    for group in (ca, ca, cb, ca, cb, cb, ca, ca, cb, ca, cb):
        step(*group)
    finish(ca)
    loss_part = gradient_piece(0)
    ga, gb = lanes_g[:3], lanes_g[3:]
    step(*ga)
    step(*cb)
    finish(cb)
    loss_part = loss_part + gradient_piece(1)
    for group in (gb, ga, ga, gb, ga, gb, ga, gb):
        step(*group)
    finish(ga)
    qg = [quarter(wg1, wq1, 0, q_send[6], q_recv[6])]
    finish(gb)
    qg.append(quarter(wg1, wq1, 1, q_send[7], q_recv[7]))

    def embed_emit(j, v, acc):
        cols = chunk_cols(j)
        grad = acc * inv_n
        u3[view_rows(v), cols] = grad
        put_stat(1, v, cols, col_sum(grad), col_sum(grad * zf[core, view_rows(v), cols].astype(F32)))

    backward_rowsplit(zf, wg1, ((0, 1),), embed_emit, at_once)
    for copy in qg:
        copy.wait_recv()
    forward_rowsplit(zf, wg1, wq1, ((1, 0),), embed_emit, at_once)
    dzf, duf = hx, zf
    stat[1, 0, zc, :, half:half + blk] = jnp.broadcast_to(loss_part, (RING, blk))
    total = stat_sum(1, half + blk)
    dgb[core, :, half:half + blk] = total[:, half:half + blk]
    copies = []
    for v in subs:
        def embed_rows(rsl, mean_g=total[first_row(v), 0:half], mean_gz=total[second_row(v), 0:half],
                       inv=sres[PAIR, second_row(v), :]):
            emb = zf[core, rsl, :].astype(F32)
            dzf[core, rsl, :] = (inv * (u3[rsl, :] - (mean_g + emb * mean_gz) * inv_n)).astype(BF16)
        apply_rows(v, embed_rows)
        copies.append(share(dzf, v))
    for copy in copies:
        copy.wait_recv()
    sent(copies + q2 + q3 + qg)

    out_recv = new_ids('r', 15)
    out_send = new_ids('s', 15)

    def publish(slot):
        up, down = device('x', 1), device('x', 3)
        sid, rid = out_send[slot * 5:slot * 5 + 5], out_recv[slot * 5:slot * 5 + 5]
        own = out_w.at[slot, core, xc]
        made = [rcopy(own, own, sid[0], rid[0], up), rcopy(own, own, sid[1], rid[1], down)]
        for copy in made:
            copy.start()
        yield
        for k, (off, target) in enumerate(((3, up), (1, down))):
            made[k].wait_recv()
            src = out_w.at[slot, core, near['x'][off], k]
            made.append(rcopy(src, src, sid[PAIR + k], rid[PAIR + k], target))
            made[-1].start()
        yield
        made[2].wait_recv()
        made[3].wait_recv()
        own = out_w.at[slot, core]
        made.append(rcopy(own, own, sid[RING], rid[RING], peer))
        made[-1].start()
        yield
        made[-1].wait_recv()
        sent(made)

    def result(slot, buf, group):
        finish(group)
        out_w[slot, core, xc] = buf[zc, yc, xc]
        yield
        yield from publish(slot)

    def layer_emit(src, slot, parity, k):
        def emit(j, v, acc):
            cols = chunk_cols(j)
            norm = (src[view_rows(v), cols] - sres[slot, first_row(v), cols]) * sres[slot, second_row(v), cols]
            lin = sres[3, row(k), cols] * norm + sres[3, row(k + 1), cols]
            grad = jnp.where(lin > 0, acc, 0.0)
            u3[view_rows(v), cols] = grad
            put_stat(parity, v, cols, col_sum(grad), col_sum(grad * norm))
        return emit

    def layer_rows(src, slot, k, total, v, store):
        sum_lin, sum_norm = total[first_row(v), 0:half], total[second_row(v), 0:half]
        mean, inv = sres[slot, first_row(v), :], sres[slot, second_row(v), :]
        scale = sres[3, row(k), :] * inv

        def fn(rsl):
            norm = (src[rsl, :] - mean) * inv
            store(rsl, (scale * (u3[rsl, :] - (sum_lin + norm * sum_norm) * inv_n)).astype(BF16))
        apply_rows(v, fn)

    def affine_grads(total, k):
        dgb[core, row(k), 0:half] = total[second_row(0), 0:half] + total[second_row(1), 0:half]
        dgb[core, row(k + 1), 0:half] = total[first_row(0), 0:half] + total[first_row(1), 0:half]

    lanes_3 = scatter_lanes(part, 0, send_a, scatter_recv[0], give=True)
    lanes_2 = scatter_lanes(part2, 1, send_b, scatter_recv[1], take=True)
    a3, b3 = lanes_3[:3], lanes_3[3:]
    a2, b2 = lanes_2[:3], lanes_2[3:]

    partial_rowsplit(part, xf2, all_rows, dzf, all_rows)
    step(*a3)
    step(*a3)
    backward_rowsplit(dzf, wg3, both, layer_emit(u2, 1, 0, PAIR), at_once)
    total = stat_sum(0, half, (a3, b3, b3))
    affine_grads(total, 0)
    copies = []
    for v in subs:
        def put_du2(rsl, value):
            duf[core, rsl, :] = value
        layer_rows(u2, 1, PAIR, total, v, put_du2)
        copies.append(share(duf, v))
    step(*b3)
    step(*a3)
    for copy in q2:
        copy.wait_recv()
    backward_colsplit(duf, wg2, wq2, layer_emit(u1, 0, 1, 0), received(copies))
    sent(copies)
    step(*a3)

    def later(fn, *args):
        fn(*args)
        yield

    total = stat_sum(1, half, ((*b3, later(partial_colsplit, part2, xf1, duf, 0)),
                               (*a3, *b3, later(partial_colsplit, part2, xf1, duf, 1)),
                               (*a2,)))
    affine_grads(total, PAIR)
    dg_send, dg_recv = new_ids('s', 1)[0], new_ids('r', 1)[0]
    dg_copy = rcopy(dgb.at[core], dgb.at[core], dg_send, dg_recv, peer)
    dg_copy.start()

    for v in subs:
        def put_du1(rsl, value, v=v):
            start = rsl.start - v * vrows
            r = pl.multiple_of(lax.rem(start, rows), min(rstep, rows))
            c = lax.div(start, rows)
            for i in range(8):
                du1[i // RING, i % RING, c, v, pl.ds(r, rstep), :] = value[:, i * blk:(i + 1) * blk]
        layer_rows(u1, 0, 0, total, v, put_du1)

    a2a_recv, a2a_send = new_ids('r', 16), new_ids('s', 16)
    targets = [(i // RING, i % RING, c) for i in range(8) for c in subs]

    own_half = lax.div(mid, 8)
    self_out = jnp.where(own_half == core, PAIR * (mid - 8 * core) + core, -1)
    self_in = jnp.where(own_half == core, mid, -1)
    a2a_home, a2a_sem = a2a.at[zc, yc], rsem.at[a2a_recv[0] + mid]

    for k, (zi, yy, c) in enumerate(targets):
        src = du1.at[zi, yy, c]

        @pl.when(self_out == k)
        def _():
            a2a_home[...] = src[...]

        @pl.when(self_out != k)
        def _():
            pltpu.make_async_remote_copy(
                src_ref=src, dst_ref=a2a_home, send_sem=ssem.at[a2a_send[k]], recv_sem=a2a_sem,
                device_id=(8 * core + zi * RING + yy, x_base + c), device_id_type=MESH_ID).start()

    slots = (hx, zf, xf1, xf2)
    per = RING * rows

    def h_fetch(chunk):
        at = chunk % RING
        made = [pltpu.make_async_copy((h_a, h_b)[chunk // RING].at[pl.ds(at * per, per), pl.ds(kh * half, half)],
                                      slots[at].at[kh], hsem.at[at * PAIR + kh]) for kh in subs]
        for copy in made:
            copy.start()
        return made

    fetches = [h_fetch(chunk) for chunk in range(RING)]
    step(*a2)
    step(*b2)
    for i in range(16):
        @pl.when(self_in != i)
        def _():
            pltpu.make_async_copy(a2a.at[i // RING, i % RING], a2a.at[i // RING, i % RING],
                                  rsem.at[a2a_recv[i]]).wait()
    step(*a2)
    step(*b2)
    for chunk in range(8):
        v, at = chunk // RING, chunk % RING
        for copy in fetches[chunk]:
            copy.wait()
        grad = jnp.concatenate([a2a[at, i, v] for i in range(RING)], axis=0)
        for kh in subs:
            for q in range(RING):
                res = dot_tn(grad, slots[at][kh, :, q * quad:(q + 1) * quad])
                spot = (slice(kh * blk, (kh + 1) * blk), slice(q * quad, (q + 1) * quad))
                u2[spot] = res + u2[spot] if chunk else res
        if chunk < RING:
            fetches.append(h_fetch(chunk + RING))
    for k, (zi, yy, c) in enumerate(targets):
        @pl.when(self_out != k)
        def _():
            pltpu.make_async_copy(du1.at[zi, yy, c], du1.at[zi, yy, c], ssem.at[a2a_send[k]]).wait()

    x_recv, x_send = new_ids('r', RING), new_ids('s', RING)
    def strip(k, cols=pl.ds(0, half)):
        return u2.at[pl.ds(pl.multiple_of(k * blk, blk), blk), cols]

    swap = rcopy(strip(other), strip(PAIR), x_send[0], x_recv[0], peer)
    swap.start()
    step(*b2)
    step(*a2)
    pub3 = result(2, part, a3 + b3)
    step(pub3)
    swap.wait_recv()
    swap.wait_send()
    strip(core)[...] = strip(core)[...] + strip(PAIR)[...]
    shifts = [rcopy(strip(core, chunk_cols(near['x'][off])), strip(3, chunk_cols(off)), x_send[off], x_recv[off],
                    device('x', off)) for off in OTHERS]
    for copy in shifts:
        copy.start()
    step(pub3)
    step(*b2)
    step(*a2)
    for copy in shifts:
        copy.wait_recv()
    got = [strip(3, chunk_cols(off))[...] for off in OTHERS]
    piece_sum = (strip(core, chunk_cols(xc))[...] + got[0]) + (got[1] + got[2])
    for s in subs:
        out_w[0, core, xc, s] = piece_sum[:, s * blk:(s + 1) * blk].T
    sent(shifts)
    pub1 = publish(0)
    step(pub1)
    step(pub3)
    step(*b2)
    step(*a2)
    step(pub1)
    step(*b2)
    step(pub1)
    pub2 = result(1, part2, a2 + b2)
    finish([pub3, pub1, pub2])
    dg_copy.wait_recv()
    dg_copy.wait_send()
    w_copy = pltpu.make_async_copy(out_w, dw_out, lsem.at[0])
    w_copy.start()
    small_out[...] = dgb[...]
    w_copy.wait()


def split_kernel(blk, dw_ref, small_ref, loss_out, dw1_out, dw2_out, dw3_out, dg1_out, db1_out, dg2_out, db2_out,
                 stage, sem_in, sem_out):
    half = 8 * blk
    mid = lax.axis_index('model')
    loads = []
    for slot in range(3):
        loads.append(pltpu.make_async_copy(dw_ref.at[slot], stage.at[slot], sem_in.at[slot]))
        loads[-1].start()
    loss_out[...] = small_ref[0, 0:1, half:half + 1] + small_ref[1, 0:1, half:half + 1]
    for hh in range(PAIR):
        dg2_out[:, hh * half:(hh + 1) * half] = small_ref[hh, 0:1, 0:half]
        db2_out[:, hh * half:(hh + 1) * half] = small_ref[hh, 1:2, 0:half]
    mcols = pl.ds(pl.multiple_of(lax.rem(mid, 8) * blk, blk), blk)
    dg1_out[...] = small_ref[lax.div(mid, 8), 2:3, mcols]
    db1_out[...] = small_ref[lax.div(mid, 8), 3:4, mcols]
    stores = []
    for slot in range(3):
        loads[slot].wait()
        for t in range(16):
            begin = pl.ds(t * blk, blk)
            dst = (dw1_out.at[begin, :], dw2_out.at[:, begin], dw3_out.at[begin, :])[slot]
            stores.append(pltpu.make_async_copy(stage.at[slot, t // 8, (t // PAIR) % RING, t % PAIR], dst,
                                                sem_out.at[len(stores)]))
            stores[-1].start()
    for copy in stores:
        copy.wait()


def build_call(blk, rows, total_rows, splits, vmem_limit):
    dim, half = 16 * blk, 8 * blk
    trows = RING * rows
    pieces = (RING, RING, RING, PAIR, blk, blk)
    got = (PAIR, RING, RING, PAIR, blk, blk)
    act = pltpu.VMEM((PAIR, trows, half), BF16)
    pre = pltpu.VMEM((trows, half), F32)
    bank = (PAIR, RING, PAIR, blk, blk)
    dma = pltpu.SemaphoreType.DMA
    scratch = [
        act, pre, pre, pre, act, act, act,
        pltpu.VMEM(pieces, BF16), pltpu.VMEM(got, BF16), pltpu.VMEM(pieces, BF16), pltpu.VMEM(got, BF16),
        pltpu.VMEM(pieces, BF16),
        pltpu.VMEM(pieces, F32), pltpu.VMEM(pieces, F32),
        pltpu.VMEM((PAIR, 6, RING, PAIR, blk, blk), F32), pltpu.VMEM((PAIR, PAIR, 6, PAIR, blk, blk), F32),
        pltpu.VMEM((PAIR, PAIR, 3, blk, blk), F32),
        pltpu.VMEM((RING, RING, 8, blk), F32),
        pltpu.VMEM((PAIR, 3, RING, RING, half + blk), F32), pltpu.VMEM((RING, RING, half), F32),
        pltpu.VMEM((PAIR, RING, half + blk), F32),
        pltpu.VMEM((PAIR, RING, PAIR, PAIR, rows, blk), BF16), pltpu.VMEM((RING, RING, PAIR, rows, blk), BF16),
        pltpu.VMEM((3,) + bank, F32),
        dma((N_SEND,)), dma((N_RECV,)), dma((16,)), dma((8,)), pltpu.SemaphoreType.REGULAR((8,)),
    ]
    anyspec = pl.BlockSpec(memory_space=pl.ANY)
    vmem = pl.BlockSpec(memory_space=pltpu.VMEM)
    smem = pl.BlockSpec(memory_space=pltpu.SMEM)
    packed = jax.ShapeDtypeStruct((3,) + bank, F32)
    step_call = pl.pallas_call(
        functools.partial(mega_kernel, (blk, rows, total_rows, splits)),
        out_shape=[packed, jax.ShapeDtypeStruct((PAIR, RING, half + blk), F32)],
        in_specs=[anyspec] * 7 + [vmem, vmem, smem],
        out_specs=[anyspec, vmem],
        scratch_shapes=scratch,
        compiler_params=pltpu.CompilerParams(collective_id=0, has_side_effects=True, vmem_limit_bytes=vmem_limit),
        name='barlow_step',
    )

    def line(n):
        return jax.ShapeDtypeStruct((1, n), F32)

    tall, wide = jax.ShapeDtypeStruct((dim, blk), F32), jax.ShapeDtypeStruct((blk, dim), F32)
    split_call = pl.pallas_call(
        functools.partial(split_kernel, blk),
        out_shape=[line(1), tall, wide, tall, line(blk), line(blk), line(dim), line(dim)],
        in_specs=[anyspec, vmem],
        out_specs=[vmem, anyspec, anyspec, anyspec, vmem, vmem, vmem, vmem],
        scratch_shapes=[pltpu.VMEM((3,) + bank, F32), dma((3,)), dma((48,))],
        name='split_results',
    )

    def call(*args):
        return split_call(*step_call(*args))

    return call


def solution(mesh):
    data_size = mesh.shape['data']

    def shard_body(h_a, h_b, w_one, w_two, w_three, g_one, b_one, g_two, b_two, lam_off):
        group_rows = h_a.shape[0]
        blk = w_three.shape[1]
        rows = group_rows // 16
        splits = ((40, 48, 40), (48, 40, 40))
        call = build_call(blk, rows, group_rows * data_size, splits, 67_000_000)
        outs = call(h_a, h_b, w_one, w_two, w_three, g_one.reshape(1, -1), b_one.reshape(1, -1),
                    g_two.reshape(1, -1), b_two.reshape(1, -1), lam_off)
        loss, dw1, dw2, dw3, dg1, db1, dg2, db2 = outs
        return (loss.reshape(1), dw1, dw2, dw3, dg1.reshape(-1), db1.reshape(-1), dg2.reshape(-1), db2.reshape(-1))

    in_specs = (P('data', None), P('data', None), P(None, 'model'), P('model', None), P(None, 'model'),
                P('model'), P('model'), P(), P(), P())
    out_specs = (P(), P(None, 'model'), P('model', None), P(None, 'model'), P('model'), P('model'), P(), P())
    return jax.shard_map(shard_body, mesh=mesh, in_specs=in_specs, out_specs=out_specs, check_vma=False)
```

time: 1390 us -> 317 us (0.23)
  waiting for transfers between devices: 1030 us -> 0 us
  Pallas kernels: 0 us -> 316 us
  blocking collectives: 136 us -> 0 us
  matrix products: 111 us -> 0 us
  other arithmetic: 72.2 us -> 0 us
    psum x4 -> x0, waiting for transfers between devices: 855 us -> none  [the longest x1 392 us: shard_body(): lax.psum(jnp.einsum('woe,ef->wof', act_one, w_two, preferred_element_type...]
    pallas_call x0 -> x2, Pallas kernels: none -> 316 us  [call(): return split_call(*step_call(*args))]
    psum x7 -> x0, blocking collectives: 136 us -> none  [the longest x3 51.2 us: batch_norm(): moments = lax.psum(local_sums, 'data') / total_rows]
    dot_general x11 -> x0, matrix products: 111 us -> none  [the longest x1 14.7 us: shard_body(): jnp.einsum('woe,wof->ef', act_two, d_out, preferred_element_type=jnp.floa...]
    reduce_scatter x1 -> x0, waiting for transfers between devices: 104 us -> none  [shard_body(): lax.psum_scatter(d_part_b, 'model', scatter_dimension=1, tiled=True)]
    all_gather x1 -> x0, waiting for transfers between devices: 72.7 us -> none  [shard_body(): emb_b_full = lax.all_gather(embed_bf[1], 'model', axis=1, tiled=True)]
    reduce_sum x6 -> x0, other arithmetic: 40.1 us -> none  [the longest x1 22 us: bn_backward(): jnp.sum(d_lin, axis=1, keepdims=True)]
    convert_element_type x3 -> x0, other arithmetic: 31.4 us -> none  [the longest x1 29.1 us: bn_backward(): d_pre.astype(jnp.bfloat16)]
  transfers between devices with their start and end apart: 6 -> 0, of which waited for: 6 -> 0; matrix products, arithmetic and copies ran while one was open for 2% -> 0% of each run, Pallas kernels for 0% -> 0%
where the time goes in v2:
time: 317 us
  Pallas kernels  316 us (100%)
    pallas_call x2, Pallas kernels, call(): return split_call(*step_call(*args))  316 us

profile of v2, /device:TPU:1, one launch (start us, length us, event | category | flops | bytes accessed | tf_op | source)
XLA Modules:
  0.0 317.2 jit_solution(1835692586669772397)
XLA Ops:
  1.3 311.1 %barlow_step.1 = (f32[3,2,4,2,128,128]{5,4,3,2,1,0:T(8,128)}, f32[2,4,1152]{2,1,0:T(4,128)}) custom-call(bf16[2048,2048]{1,0:T(8,128)(2,1)} %h_a.1, bf16[2048,2048]{1,0:T(8,128)(2,1)} %h_b.1, bf16[2048,128]{1,0:T(8,128)(2,1)} %w_one.1, bf16[128,2048]{1,0:T(8,128)(2,1)} %w_two.1, bf16[2048,128]{1,0:T(8,128)(2,1)} %w_three.1, f32[1,128]{1,0:T(1,128)} %bitcast.11, ...), custom_call_target="tpu_custom_call" | custom-call | tf_op jit(solution)/shard_map/barlow_step/pallas_call | solution.py:896
  312.4 4.7 %split_results.1 = (f32[1,1]{1,0:T(1,128)}, f32[2048,128]{1,0:T(8,128)}, f32[128,2048]{1,0:T(8,128)}, f32[2048,128]{1,0:T(8,128)}, f32[1,128]{1,0:T(1,128)}, /*i...) custom-call(f32[3,2,4,2,128,128]{5,4,3,2,1,0:T(8,128)} %get-tuple-element.18.dw_ref, ...), custom_call_target="tpu_custom_call" | custom-call | tf_op jit(solution)/shard_map/split_results/pallas_call | solution.py:896

commit v3 on v2

v3 whole, which is shorter than its diff:
```python
import functools

import jax
import jax.numpy as jnp
from jax import lax
from jax.experimental import pallas as pl
from jax.experimental.pallas import tpu as pltpu
from jax.sharding import PartitionSpec as P

BN_EPS = 1e-5
MESH_ID = pl.DeviceIdType.MESH
RING = 4
PAIR = 2
AXES = ('z', 'y', 'x')
ORDERS = (('x', 'y', 'z'), ('y', 'z', 'x'), ('z', 'x', 'y'))
COARSE = ((0, 0, (40, 48, 40)), (1, 0, (48, 40, 40)))
FINE = COARSE
MERGED = ((slice(PAIR), 0, (40, 48, 40)),)
BACK = COARSE
OTHERS = (1, 2, 3)
N_SEND = 520
N_RECV = 520
BYTES_PER_US = 46600.0
HOP = 1.9
TWO_HOPS = 2.7
BACKLOG = 5.0
SMALL = 60000
FAR = 1e9
F32 = jnp.float32
BF16 = jnp.bfloat16
WHOLE = slice(None)
FIRST, SECOND = 0, 1
BLOCKS, HALF_BLOCKS = 16, 8
NOW = 0.0
STEP = 0.2
STAT_SIZE = 32768


def dot_nn(a, b):
    return lax.dot_general(a, b, (((1,), (0,)), ((), ())), preferred_element_type=F32)


def dot_nt(a, b):
    return lax.dot_general(a, b, (((1,), (1,)), ((), ())), preferred_element_type=F32)


def dot_tn(a, b):
    return lax.dot_general(a, b, (((0,), (0,)), ((), ())), preferred_element_type=F32)


def col_sum(value):
    return jnp.sum(value, axis=0, keepdims=True)


def lanes_of(values):
    return jnp.concatenate(list(values), axis=1)


def wrap(value):
    return lax.rem(value, RING)


class Plan:
    def __init__(self):
        self.now = 0.0
        self.free = dict.fromkeys(AXES, 0.0)
        self.need = dict.fromkeys(AXES, FAR)
        self.lanes = []
        self.first = None

    def work(self, us):
        self.now += us

    def until(self, when):
        self.now = max(self.now, when)

    def send(self, axis, size, flight=HOP):
        self.free[axis] = max(self.free[axis], self.now) + size / BYTES_PER_US
        return self.free[axis] + flight

    def add(self, gens, then=None, first=False):
        group = {'left': 0, 'then': then}
        made = []
        for gen in gens:
            group['left'] += 1
            made.append([gen, next(gen), group])
        self.lanes = made + self.lanes if first else self.lanes + made
        return group

    def start_of(self, lane):
        ready, loads, _ = lane[1]
        start = max(self.now, ready() if callable(ready) else ready)
        if self.first is not None and lane[2] not in self.first and max(loads.values(), default=0) > SMALL:
            return FAR
        for axis, size in loads.items():
            start = max(start, self.free[axis] - BACKLOG)
        for axis, size in loads.items():
            if max(self.free[axis], start) + size / BYTES_PER_US > self.need[axis] + 1.0:
                return FAR
        return start

    def advance(self, limit):
        best, begin = None, limit
        for lane in self.lanes:
            start = self.start_of(lane)
            if start < begin and start + lane[1][2] < limit + 1.0:
                best, begin = lane, start
        if best is None:
            return False
        self.until(begin)
        info = next(best[0], None)
        if info is not None:
            best[1] = info
            return True
        self.lanes = [lane for lane in self.lanes if lane is not best]
        group = best[2]
        group['left'] -= 1
        if not group['left'] and group['then'] is not None:
            group['then']()
        return True

    def pump(self, limit):
        while self.advance(limit):
            pass

    def finish(self, *groups, alone=False):
        self.first = groups if alone else None
        while any(group['left'] for group in groups):
            if not self.advance(FAR):
                self.need = dict.fromkeys(AXES, FAR)
        self.first = None

    def expect(self, when):
        for axis in AXES:
            self.need[axis] = when
            when += 3.6


def mega_kernel(cfg, h_a, h_b, w_one, w_two, w_three, g_one, b_one, g_two, b_two, lam_ref,
                dw_out, small_out,
                hx, u1, u2, u3, xf1, xf2, zf, wg1, wq1, wg2, wq2, wg3, part, part2, rv1, rv2, rv3,
                gbuf, stat, sres, dgb, zsum, vec, vecx, vecp, du1, a2a, out_w, ssem, rsem, lsem, hsem, credit):
    blk, rows, total_rows = cfg
    plan = Plan()
    half = HALF_BLOCKS * blk
    quad = PAIR * blk
    vrows = PAIR * rows
    inv_n = 1.0 / total_rows

    mid = lax.axis_index('model')
    did = lax.axis_index('data')
    core = lax.rem(did, PAIR)
    other = 1 - core
    coord = {'z': lax.div(mid, RING), 'y': wrap(mid), 'x': lax.div(did, PAIR)}
    zc, yc, xc = coord['z'], coord['y'], coord['x']
    near = {axis: [coord[axis]] + [wrap(coord[axis] + off) for off in OTHERS] for axis in AXES}
    z_base, x_base = zc * RING, xc * PAIR
    targets_of = {'z': [(q * RING + yc, did) for q in near['z']], 'y': [(z_base + q, did) for q in near['y']],
                  'x': [(mid, q * PAIR + core) for q in near['x']]}
    peer = (mid, x_base + other)

    def device(axis, off):
        return targets_of[axis][off]

    z_own, z_other = PAIR * core, PAIR * other
    counters = {'s': 0, 'r': 0, 'l': 0}

    def new_ids(kind, count):
        first = counters[kind]
        counters[kind] = first + count
        assert counters[kind] <= {'s': N_SEND, 'r': N_RECV, 'l': BLOCKS}[kind]
        return list(range(first, first + count))

    def rcopy(src, dst, send_id, recv_id, target):
        return pltpu.make_async_remote_copy(src_ref=src, dst_ref=dst, send_sem=ssem.at[send_id],
                                            recv_sem=rsem.at[recv_id], device_id=target, device_id_type=MESH_ID)

    def bands(batches):
        for sub, begin, sizes in batches:
            for colour, size in enumerate(sizes):
                yield sub, colour, pl.ds(begin, size), size * blk * (PAIR if isinstance(sub, slice) else 1)
                begin += size

    def gather_lane(buf, sub, colour, rsl, cells, sid, rid):
        order = ORDERS[colour]
        size = PAIR * cells

        def region(axis, have, q, part_id=None):
            idx = dict(coord)
            idx[axis] = q
            for name in have:
                idx[name] = WHOLE
            if part_id is not None:
                idx[have[-1]] = pl.ds(PAIR * part_id, PAIR)
            return buf.at[idx['z'], idx['y'], idx['x'], sub, rsl, :]

        axis = order[0]
        yield NOW, {axis: PAIR * size}, NOW
        own = region(axis, (), coord[axis])
        pending = [rcopy(own, own, sid[off - 1], rid[off - 1], device(axis, off)) for off in OTHERS]
        for copy in pending:
            copy.start()
        ready = plan.send(axis, PAIR * size, TWO_HOPS)
        for phase in (1, 2):
            size *= RING
            axis, have = order[phase], order[:phase]
            yield ready, {axis: size}, STEP
            for copy in pending[-3:] if phase == 1 else pending[-2:]:
                copy.wait_recv()
            base = phase * RING - 1
            up, down = device(axis, 1), device(axis, 3)
            own = region(axis, have, coord[axis])
            to_up = rcopy(own, own, sid[base], rid[base], up)
            to_down = rcopy(own, own, sid[base + 1], rid[base + 1], down)
            to_up.start()
            to_down.start()
            yield plan.send(axis, size), {axis: size / PAIR}, STEP
            to_up.wait_recv()
            src = region(axis, have, near[axis][3], 0)
            relay_up = rcopy(src, src, sid[base + 2], rid[base + 2], up)
            relay_up.start()
            to_down.wait_recv()
            src = region(axis, have, near[axis][1], 1)
            relay_down = rcopy(src, src, sid[base + 3], rid[base + 3], down)
            relay_down.start()
            ready = plan.send(axis, size / PAIR)
            pending.extend((to_up, to_down, relay_up, relay_down))
        yield ready, {}, STEP
        for copy in pending[-2:]:
            copy.wait_recv()
        for copy in pending:
            copy.wait_send()

    def lanes_by_batch(make, batches, send_ids, recv_ids, width):
        lanes = []
        for k, found in enumerate(bands(batches)):
            ids = slice(k * width, (k + 1) * width)
            lanes.append(make(k, *found, send_ids[ids], recv_ids[ids]))
        return [lanes[k:k + 3] for k in range(0, len(lanes), 3)]

    def gather_lanes(buf, batches, send_ids, recv_ids):
        return lanes_by_batch(lambda k, *args: gather_lane(buf, *args), batches, send_ids, recv_ids, 11)

    given = {}

    def scatter_lane(buf, bank, give, take, sub, colour, rsl, cells, sid, rid):
        order = ORDERS[colour]
        pending = []
        ready = NOW
        size = cells * 32
        for phase in (0, 1):
            axis = order[phase]
            left = tuple(name for name in AXES if name in order[phase + 1:])
            p = coord[axis]
            base = phase * 6

            def region(q, part_id, axis=axis, left=left):
                idx = dict(coord)
                idx[axis] = q
                for name in left[:-1]:
                    idx[name] = WHOLE
                idx[left[-1]] = pl.ds(PAIR * part_id, PAIR)
                return buf.at[idx['z'], idx['y'], idx['x'], sub, rsl, :]

            def landing(slot, phase=phase):
                if phase:
                    return rv2.at[bank, sub, slot, :, rsl, :]
                return rv1.at[sub, slot, :, :, rsl, :]

            def add(q, part_id, slots, axis=axis, left=left, phase=phase):
                def one(i, j):
                    idx = dict(coord)
                    idx[axis] = q
                    idx[left[-1]] = PAIR * part_id + j
                    if not phase:
                        idx[left[0]] = i
                    total = buf[idx['z'], idx['y'], idx['x'], sub, rsl, :]
                    for slot in slots:
                        total = total + (rv2[bank, sub, slot, j, rsl, :] if phase else rv1[sub, slot, i, j, rsl, :])
                    buf[idx['z'], idx['y'], idx['x'], sub, rsl, :] = total

                if phase:
                    for j in range(PAIR):
                        one(0, j)
                else:
                    @pl.loop(0, RING)
                    def _(i):
                        for j in range(PAIR):
                            one(i, j)

            up, down = device(axis, 1), device(axis, 3)
            p1, p2, p3 = near[axis][1:]
            if phase:
                yield ready, {axis: PAIR * size}, STEP
                finals()
            else:
                yield (ready if take is None else lambda: given.get(take, FAR)), {axis: size}, NOW
                if take is not None:
                    pl.semaphore_wait(credit.at[take], PAIR)
            relay_up = rcopy(region(p2, 1), landing(0), sid[base], rid[base], up)
            relay_down = rcopy(region(p2, 0), landing(1), sid[base + 1], rid[base + 1], down)
            own_up = rcopy(region(p1, 0), landing(2), sid[base + 2], rid[base + 2], up)
            own_down = rcopy(region(p3, 1), landing(3), sid[base + 3], rid[base + 3], down)
            relay_up.start()
            relay_down.start()
            relayed = plan.send(axis, size)
            if not phase:
                yield NOW, {axis: size}, NOW
            own_up.start()
            own_down.start()
            plan.send(axis, size)
            yield relayed, {axis: size}, STEP
            relay_up.wait_recv()
            add(p1, 1, (0,))
            sum_up = rcopy(region(p1, 1), landing(4), sid[base + 4], rid[base + 4], up)
            sum_up.start()
            relay_down.wait_recv()
            add(p3, 0, (1,))
            sum_down = rcopy(region(p3, 0), landing(5), sid[base + 5], rid[base + 5], down)
            sum_down.start()
            ready = plan.send(axis, size)
            size /= RING

            def finals(phase=phase, p=p, add=add, own_up=own_up, own_down=own_down, sum_up=sum_up, sum_down=sum_down,
                       up=up, down=down):
                own_up.wait_recv()
                sum_down.wait_recv()
                add(p, 0, (2, 5))
                own_down.wait_recv()
                sum_up.wait_recv()
                add(p, 1, (3, 4))
                if give is not None and not phase:
                    given[give] = plan.now + 1.0
                    for target in (up, down):
                        pl.semaphore_signal(credit.at[give], device_id=target, device_id_type=MESH_ID)

            pending.extend((relay_up, relay_down, own_up, own_down, sum_up, sum_down))
        axis = order[2]
        size *= RING
        yield ready, {axis: size}, STEP
        finals()
        base = 12
        last = []
        for k, off in enumerate(OTHERS):
            idx = dict(coord)
            idx[axis] = near[axis][off]
            last.append(rcopy(buf.at[idx['z'], idx['y'], idx['x'], sub, rsl, :], rv3.at[bank, sub, k, rsl, :],
                              sid[base + k], rid[base + k], device(axis, off)))
        for copy in last:
            copy.start()
        yield plan.send(axis, size, TWO_HOPS), {}, STEP
        for copy in last:
            copy.wait_recv()
        got = [rv3[bank, sub, k, rsl, :] for k in range(3)]
        buf[zc, yc, xc, sub, rsl, :] = (buf[zc, yc, xc, sub, rsl, :] + got[0]) + (got[1] + got[2])
        for copy in pending + last:
            copy.wait_send()

    def scatter_lanes(buf, bank, batches, send_ids, recv_ids, give=False, take=False):
        return lanes_by_batch(lambda k, *args: scatter_lane(buf, bank, k if give else None, k if take else None, *args),
                              batches, send_ids, recv_ids, 15)

    released = []

    def quarter(src, dst, batch, send_id, recv_id, made, held=None):
        sub, begin, sizes = batch
        rsl = pl.ds(begin, sum(sizes))

        def send():
            if held is not None and not released:
                held.append(send)
                return
            copy = rcopy(src.at[pl.ds(z_other, PAIR), :, :, sub, rsl, :], dst.at[:, :, :, sub, rsl, :], send_id, recv_id,
                         peer)
            copy.start()
            made.append(copy)
        return send

    stat_recv = [new_ids('r', 9) for _ in range(PAIR)]
    stat_send = new_ids('s', 9)

    def stat_steps(parity, out):
        pending, ready, width = [], NOW, slice(half)
        for d, axis in enumerate(AXES):
            yield ready, {axis: STAT_SIZE}, STEP
            if d:
                stat[parity, d, coord[axis], :, width] = gathered_stat(parity, d - 1, pending)
            own = stat.at[parity, d, coord[axis], :, width]
            copies = [rcopy(own, own, stat_send[d * 3 + off - 1], stat_recv[parity][d * 3 + off - 1], device(axis, off))
                      for off in OTHERS]
            for copy in copies:
                copy.start()
            pending.extend(copies)
            ready = plan.send(axis, STAT_SIZE, TWO_HOPS)
        yield ready, {}, STEP
        out.append(gathered_stat(parity, d, pending))
        for copy in pending:
            copy.wait_send()

    def gathered_stat(parity, d, pending):
        for copy in pending[-3:]:
            copy.wait_recv()
        got = [stat[parity, d, q, :, :half] for q in range(RING)]
        return (got[0] + got[1]) + (got[PAIR] + got[3])

    def stat_sum(parity):
        out = []
        steps = stat_steps(parity, out)
        next(steps)
        plan.expect(plan.now)
        for axis in AXES:
            ready = next(steps)[0]
            plan.need[axis] = FAR
            plan.pump(ready)
            plan.until(ready)
            plan.work(STEP)
        next(steps, None)
        return out[0]

    def row(k):
        return slice(k, k + 1)

    def first_row(v):
        return row(PAIR * v)

    def second_row(v):
        return row(PAIR * v + 1)

    def put_stat(parity, v, cols, first, second):
        stat[parity, 0, zc, first_row(v), cols] = first
        stat[parity, 0, zc, second_row(v), cols] = second

    def local(src, dst):
        copy = pltpu.make_async_copy(src, dst, lsem.at[new_ids('l', 1)[0]])
        copy.start()
        return copy

    row0 = pl.multiple_of(core * half + xc * quad, quad)
    subs = range(PAIR)
    w1_loads = [local(w_one.at[pl.ds(row0 + s * blk, blk), :], wg1.at[zc, yc, xc, s]) for s in subs]
    hrow = pl.multiple_of(mid * rows, rows)
    h_ids = [new_ids('s', RING), new_ids('r', RING)]
    h_pairs = []
    for v, h_ref in enumerate((h_a, h_b)):
        for kh in subs:
            h_pairs.append((h_ref.at[pl.ds(hrow, rows), pl.ds(kh * half, half)],
                            hx.at[kh, pl.ds(pl.multiple_of(v * vrows + core * rows, rows), rows), :]))
    more_loads = [local(src, dst) for src, dst in h_pairs]
    more_loads.append(local(g_one, gbuf.at[zc, yc, row(FIRST), :]))
    more_loads.append(local(b_one, gbuf.at[zc, yc, row(SECOND), :]))
    for s in subs:
        more_loads.append(local(w_two.at[:, pl.ds(row0 + s * blk, blk)], wg2.at[zc, yc, xc, s]))
        more_loads.append(local(w_three.at[pl.ds(row0 + s * blk, blk), :], wg3.at[zc, yc, xc, s]))

    barrier = pltpu.get_barrier_semaphore()
    greeted = [device(axis, off) for axis in AXES for off in OTHERS] + [peer]
    for target in greeted:
        pl.semaphore_signal(barrier, device_id=target, device_id_type=MESH_ID)
    pl.semaphore_wait(barrier, len(greeted))

    width = 66
    send_w = [new_ids('s', width) for _ in range(3)]
    recv_w = [new_ids('r', width) for _ in range(3)]
    send_w_all, recv_w_all = sum(send_w, []), sum(recv_w, [])
    send_g, recv_c = new_ids('s', 180), new_ids('r', 180)
    q_send, q_recv = new_ids('s', 10), new_ids('r', 10)
    q1, q2, q3, qg, held3 = [], [], [], [], []

    def add_gather(buf, dst, batches, send_ids, recv_ids, quarter_at, made, held=None):
        return [plan.add(lanes, quarter(buf, dst, batch, q_send[quarter_at + k], q_recv[quarter_at + k], made, held))
                for k, (batch, lanes) in enumerate(zip(batches, gather_lanes(buf, batches, send_ids, recv_ids)))]

    gb_recv = new_ids('r', 6)

    def gain_lane():
        ready, sent_copies = NOW, []
        for k, axis, own in ((0, 'y', gbuf.at[zc, yc]), (3, 'z', gbuf.at[zc])):
            yield ready, {axis: STAT_SIZE}, NOW
            for copy in sent_copies:
                copy.wait_recv()
            made = [rcopy(own, own, stat_send[k + off - 1], gb_recv[k + off - 1], device(axis, off)) for off in OTHERS]
            for copy in made:
                copy.start()
            ready = plan.send(axis, STAT_SIZE, TWO_HOPS)
            sent_copies.extend(made)
        yield ready, {}, NOW
        for copy in made:
            copy.wait_recv()
        for copy in sent_copies:
            copy.wait_send()

    for copy in w1_loads:
        copy.wait()
    gather1 = add_gather(wg1, wq1, COARSE, send_w[0], recv_w[0], 0, q1)
    plan.pump(0.1)
    h_copies = [rcopy(src, dst, h_ids[0][k], h_ids[1][k], peer) for k, (src, dst) in enumerate(h_pairs)]
    for copy in h_copies:
        copy.start()
    for copy in more_loads:
        copy.wait()
    gather1.append(plan.add([gain_lane()], first=True))
    gather2 = add_gather(wg2, wq2, MERGED, send_w[1], recv_w[1], PAIR, q2)
    plan.finish(*gather1, alone=True)
    gather3 = add_gather(wg3, wq1, MERGED, send_w[PAIR], recv_w[PAIR], RING, q3, held3)
    for copy in h_copies:
        copy.wait_recv()
    plan.pump(plan.now + STEP)
    for copy in q1:
        copy.wait_recv()
    plan.work(PAIR)

    def gathered(k):
        return lanes_of(gbuf[z, i, row(k), :] for z in (z_own, z_own + 1) for i in range(RING))

    gain1, shift1 = gathered(0), gathered(1)
    my_cols = pl.ds(pl.multiple_of(core * half, half), half)
    gain2, shift2 = g_two[:, my_cols], b_two[:, my_cols]
    for k, value in enumerate((gain1, shift1, gain2, shift2)):
        sres[3, row(k), :] = value

    def view_rows(v):
        return pl.ds(v * vrows, vrows)

    def chunk_cols(j):
        return pl.ds(pl.multiple_of(j * quad, quad), quad)

    def over_chunks(fn):
        pl.loop(0, RING)(fn)

    def forward_rowsplit(act, own, got, views, emit, ready):
        for v, src_v in views:
            ready[v]()

            def body(j):
                zz, y0 = lax.div(j, PAIR), lax.rem(j, PAIR) * PAIR
                sides = [lanes_of(ref[z, yy].reshape(half, blk) for yy in (y0, y0 + 1))
                         for ref, z in ((own, z_own + zz), (got, zz))]
                emit(j, v, dot_nn(act[core, view_rows(src_v), :], sides[0])
                     + dot_nn(act[other, view_rows(src_v), :], sides[1]))
            over_chunks(body)

    def forward_colsplit(act, own, emit, ready):
        for v in subs:
            ready[v]()

            def body(j):
                sides = [lanes_of(own[PAIR * hh:PAIR * hh + PAIR, :, j, s].reshape(half, blk) for s in subs)
                         for hh in subs]
                emit(j, v, dot_nn(act[0, view_rows(v), :], sides[0]) + dot_nn(act[1, view_rows(v), :], sides[1]))
            over_chunks(body)

    def backward_rowsplit(act, own, views, emit, ready):
        for v, src_v in views:
            ready[v]()

            def body(j):
                sides = [lanes_of(own[PAIR * hh + i // RING, i % RING, j].reshape(quad, blk) for i in range(HALF_BLOCKS))
                         for hh in subs]
                emit(j, v, dot_nt(act[0, view_rows(src_v), :], sides[0])
                     + dot_nt(act[1, view_rows(src_v), :], sides[1]))
            over_chunks(body)

    def backward_colsplit(act, own, got, emit, ready):
        for v in subs:
            ready[v]()

            def body(j):
                sides = []
                zz, y0 = lax.div(j, PAIR), lax.rem(j, PAIR) * PAIR
                for ref, z in ((own, z_own + zz), (got, zz)):
                    bands = [lanes_of(ref[z, yy, t // PAIR, t % PAIR] for t in range(HALF_BLOCKS)) for yy in (y0, y0 + 1)]
                    sides.append(jnp.concatenate(bands, axis=0))
                emit(j, v, dot_nt(act[core, view_rows(v), :], sides[0]) + dot_nt(act[other, view_rows(v), :], sides[1]))
            over_chunks(body)

    def partial_rowsplit(dst, lhs, lhs_rows, rhs, rhs_rows):
        def body(j):
            left = lhs[core, lhs_rows, chunk_cols(j)]
            for hh in subs:
                for t in range(RING):
                    res = dot_tn(left, rhs[hh, rhs_rows, t * quad:(t + 1) * quad])
                    for i in subs:
                        for s in subs:
                            dst[PAIR * hh + t // PAIR, (t % PAIR) * PAIR + i, j, s] = res[s * blk:(s + 1) * blk,
                                                                                         i * blk:(i + 1) * blk]
        over_chunks(body)

    def partial_colsplit(dst, lhs, rhs, hh):
        def body(t):
            left = lhs[hh, :, chunk_cols(t)]
            zz, y0 = PAIR * hh + lax.div(t, PAIR), lax.rem(t, PAIR) * PAIR
            for q in range(RING):
                res = dot_tn(left, rhs[core, :, q * quad:(q + 1) * quad])
                for i, yy in enumerate((y0, y0 + 1)):
                    for s in subs:
                        dst[zz, yy, q, s] = res[i * blk:(i + 1) * blk, s * blk:(s + 1) * blk]
        over_chunks(body)

    def forward_emit(dst, parity):
        def emit(j, v, acc):
            cols = chunk_cols(j)
            dst[view_rows(v), cols] = acc
            put_stat(parity, v, cols, col_sum(acc), col_sum(acc * acc))
        return emit

    def moments(total, slot):
        for v in subs:
            mean = total[first_row(v), :half] * inv_n
            inv = lax.rsqrt(total[second_row(v), :half] * inv_n - mean * mean + BN_EPS)
            sres[slot, first_row(v), :] = mean
            sres[slot, second_row(v), :] = inv

    act_send, act_recv = new_ids('s', PAIR), new_ids('r', 10)

    def share(dst, v):
        region = dst.at[core, view_rows(v), :]
        copy = rcopy(region, region, act_send[v], act_recv.pop(), peer)
        copy.start()
        return copy

    rstep = min(32, vrows)

    def apply_rows(v, fn):
        @pl.loop(0, vrows // rstep)
        def _(i):
            fn(pl.ds(pl.multiple_of(v * vrows + i * rstep, rstep), rstep))

    def activate(src, slot, gain, shift, dst):
        copies = []
        for v in subs:
            mean = sres[slot, first_row(v), :]
            inv = sres[slot, second_row(v), :]

            def fn(rsl, mean=mean, inv=inv):
                norm = (src[rsl, :] - mean) * inv
                if gain is not None:
                    norm = jnp.maximum(gain * norm + shift, NOW)
                dst[core, rsl, :] = norm.astype(BF16)
            apply_rows(v, fn)
            copies.append(share(dst, v))
        plan.work(1)
        plan.pump(plan.now + PAIR)
        return copies

    def received(copies):
        return [copy.wait_recv for copy in copies]

    def sent(copies):
        for copy in copies:
            copy.wait_send()

    def nothing():
        pass

    both = ((0, 0), (1, 1))
    at_once = (nothing, nothing)
    all_rows = pl.ds(0, PAIR * vrows)

    MM = 3.7

    def product(fn, *args):
        plan.expect(plan.now + MM)
        plan.pump(plan.now + STEP)
        fn(*args)
        plan.work(MM)

    product(forward_rowsplit, hx, wg1, wq1, both, forward_emit(u1, 0), at_once)
    moments(stat_sum(0), 0)
    copies = activate(u1, 0, gain1, shift1, xf1)
    sent(q1 + h_copies)
    plan.finish(*gather2)
    product(forward_colsplit, xf1, wg2, forward_emit(u2, 1), received(copies))
    released.append(True)
    for send in held3:
        send()
    sent(copies)
    moments(stat_sum(1), 1)
    copies = activate(u2, 1, gain2, shift2, xf2)
    plan.finish(*gather3)
    for copy in q3:
        copy.wait_recv()
    product(forward_rowsplit, xf2, wg3, wq1, both, forward_emit(u3, 0), received(copies))
    sent(copies)
    moments(stat_sum(0), PAIR)
    copies = activate(u3, PAIR, None, None, zf)
    for copy in copies:
        copy.wait_recv()
    sent(copies)

    for v in subs:
        stat[1, 0, zc, row(v), :half] = col_sum(zf[core, view_rows(v), :].astype(F32))
    zsum_ids = new_ids('s', 1) + new_ids('r', 1)

    def zsum_lane():
        out = []
        yield from stat_steps(1, out)
        zsum[core] = out[0]
        copy = rcopy(zsum.at[core], zsum.at[core], *zsum_ids, peer)
        copy.start()
        yield plan.now + PAIR, {}, NOW
        copy.wait_recv()
        copy.wait_send()

    zsum_group = plan.add([zsum_lane()], first=True)

    partial_rowsplit(part, zf, view_rows(0), zf, view_rows(1))
    lam = lam_ref[0]
    losses = []

    def gradient_of(k, batch):
        def go():
            sub, begin, sizes = batch
            count = sum(sizes)
            rsl = pl.ds(begin, count)
            corr = part[zc, yc, xc, sub, rsl, :] * inv_n
            row_ids = (core * half + xc * quad + (sub * blk + begin)) + lax.broadcasted_iota(jnp.int32, (count, blk), 0)
            diag = row_ids == mid * blk + lax.broadcasted_iota(jnp.int32, (count, blk), 1)
            terms = jnp.where(diag, (1.0 - corr) * (1.0 - corr), lam * corr * corr)
            losses.append(jnp.sum(col_sum(terms), axis=1, keepdims=True))
            wg1[zc, yc, xc, sub, rsl, :] = jnp.where(diag, -2.0 * (1.0 - corr), 2.0 * lam * corr).astype(BF16)
            gather_g.append(plan.add(lanes_g[k], quarter(wg1, wq1, batch, q_send[6 + k], q_recv[6 + k], qg)))
        return go

    gather_g = []
    lanes_g = gather_lanes(wg1, FINE, send_g, recv_w_all)
    scatter_c = [plan.add(lanes, gradient_of(k, FINE[k]))
                 for k, lanes in enumerate(scatter_lanes(part, 0, FINE, send_w_all, recv_c))]
    plan.finish(zsum_group, *scatter_c)

    share_of = []
    sum_b = zsum[lax.div(mid, HALF_BLOCKS), row(SECOND), pl.ds(pl.multiple_of(lax.rem(mid, HALF_BLOCKS) * blk, blk), blk)]
    for s in subs:
        grad = wg1[zc, yc, xc, s].astype(F32)
        both_terms = grad * (part[zc, yc, xc, s] * inv_n)
        sum_a = zsum[core, row(FIRST), pl.ds(pl.multiple_of(xc * quad + s * blk, blk), blk)]
        share_of.append((col_sum((grad.T * sum_a).T) * inv_n, col_sum(both_terms), col_sum((grad * sum_b).T) * inv_n,
                         col_sum(both_terms.T)))
    (c0, c1, r00, r10), (d0, d1, r01, r11) = share_of
    loss_row = jnp.broadcast_to(sum(losses[1:], losses[0]), (1, blk))
    vec[zc, yc] = jnp.concatenate([c0 + d0, c1 + d1, r00, r01, r10, r11, loss_row, loss_row], axis=0)
    vec_send, vec_recv = new_ids('s', 10), new_ids('r', 10)

    def vec_lane():
        ready, pending = NOW, []
        for k, axis in enumerate(AXES[::-1][1:] + AXES[PAIR:]):
            yield ready, {axis: STAT_SIZE}, STEP
            for copy in pending[-3:]:
                copy.wait_recv()
            if axis == 'x':
                plane = [vec[t // RING, t % RING] for t in range(BLOCKS)]
                rest_rows = sum(plane[1:], plane[0])
                vecx[xc] = jnp.concatenate([item[:PAIR] for item in plane] + [rest_rows], axis=0)
            own = {'y': vec.at[zc, yc], 'z': vec.at[zc], 'x': vecx.at[xc]}[axis]
            made = [rcopy(own, own, vec_send[k * 3 + off - 1], vec_recv[k * 3 + off - 1], device(axis, off))
                    for off in OTHERS]
            for copy in made:
                copy.start()
            ready = plan.send(axis, STAT_SIZE, TWO_HOPS)
            pending.extend(made)
        yield ready, {}, STEP
        for copy in made:
            copy.wait_recv()
        got = [vecx[q] for q in range(RING)]
        vecp[core] = (got[0] + got[1]) + (got[PAIR] + got[3])
        copy = rcopy(vecp.at[core], vecp.at[core], vec_send[9], vec_recv[9], peer)
        copy.start()
        yield plan.now + PAIR, {}, NOW
        copy.wait_recv()
        sent(pending + [copy])

    vec_group = plan.add([vec_lane()], first=True)
    plan.finish(*gather_g)

    def embed_emit(j, v, acc):
        u3[view_rows(v), chunk_cols(j)] = acc * inv_n

    backward_rowsplit(zf, wg1, ((0, 1),), embed_emit, at_once)
    for copy in qg:
        copy.wait_recv()
    forward_rowsplit(zf, wg1, wq1, ((1, 0),), embed_emit, at_once)
    dzf, duf = hx, zf
    plan.work(MM)
    plan.finish(vec_group)
    first_r = PAIR * BLOCKS + PAIR
    dgb[core, :, half:half + blk] = jnp.broadcast_to(vecp[core, row(first_r + RING), :], (RING, blk))
    mine = pl.ds(pl.multiple_of(BLOCKS * core, BLOCKS), BLOCKS)
    both_cores = vecp[0, mine, :] + vecp[1, mine, :]
    sums = [[lanes_of(vecx[q, row(first_r + PAIR * t + s), :] for q in range(RING) for s in subs) for t in subs],
            [lanes_of(both_cores[row(PAIR * i + t)] for i in range(HALF_BLOCKS)) for t in subs]]
    copies = []
    for v in subs:
        def embed_rows(rsl, mean_g=sums[v][0], mean_gz=sums[v][1], inv=sres[PAIR, second_row(v), :]):
            emb = zf[core, rsl, :].astype(F32)
            dzf[core, rsl, :] = (inv * (u3[rsl, :] - (mean_g + emb * mean_gz) * inv_n)).astype(BF16)
        apply_rows(v, embed_rows)
        copies.append(share(dzf, v))
    for copy in copies:
        copy.wait_recv()
    sent(copies + q2 + q3 + qg)

    out_ids = {(slot, s): (new_ids('s', 5), new_ids('r', 5)) for slot in range(3) for s in subs}

    def publish(slot, s):
        size = PAIR * blk * blk * PAIR
        up, down = device('x', 1), device('x', 3)
        sid, rid = out_ids[slot, s]
        own = out_w.at[slot, core, xc, s]
        made = [rcopy(own, own, sid[FIRST], rid[FIRST], up), rcopy(own, own, sid[SECOND], rid[SECOND], down)]
        yield NOW, {'x': size}, NOW
        for copy in made:
            copy.start()
        yield plan.send('x', size), {'x': size / PAIR}, NOW
        for k, (off, target) in enumerate(((3, up), (1, down))):
            made[k].wait_recv()
            src = out_w.at[slot, core, near['x'][off], s, pl.ds(k * blk // PAIR, blk // PAIR), :]
            made.append(rcopy(src, src, sid[PAIR + k], rid[PAIR + k], target))
            made[-1].start()
        yield plan.send('x', size / PAIR), {}, NOW
        made[PAIR].wait_recv()
        made[3].wait_recv()
        own = out_w.at[slot, core, :, s]
        made.append(rcopy(own, own, sid[RING], rid[RING], peer))
        made[-1].start()
        yield plan.now + PAIR, {}, NOW
        made[-1].wait_recv()
        sent(made)

    published = []

    def result(slot, buf, s, groups):
        def go():
            if not any(group['left'] for group in groups):
                out_w[slot, core, xc, s] = buf[zc, yc, xc, s]
                published.append(plan.add([publish(slot, s)], first=True))
        return go

    def layer_emit(src, slot, parity, k):
        def emit(j, v, acc):
            cols = chunk_cols(j)
            norm = (src[view_rows(v), cols] - sres[slot, first_row(v), cols]) * sres[slot, second_row(v), cols]
            lin = sres[3, row(k), cols] * norm + sres[3, row(k + 1), cols]
            grad = jnp.where(lin > 0, acc, NOW)
            u3[view_rows(v), cols] = grad
            put_stat(parity, v, cols, col_sum(grad), col_sum(grad * norm))
        return emit

    def layer_rows(src, slot, k, total, v, store):
        sum_lin, sum_norm = total[first_row(v), :half], total[second_row(v), :half]
        mean, inv = sres[slot, first_row(v), :], sres[slot, second_row(v), :]
        scale = sres[3, row(k), :] * inv

        def fn(rsl):
            norm = (src[rsl, :] - mean) * inv
            store(rsl, (scale * (u3[rsl, :] - (sum_lin + norm * sum_norm) * inv_n)).astype(BF16))
        apply_rows(v, fn)

    def affine_grads(total, k):
        dgb[core, row(k), :half] = total[second_row(FIRST), :half] + total[second_row(SECOND), :half]
        dgb[core, row(k + 1), :half] = total[first_row(FIRST), :half] + total[first_row(SECOND), :half]

    def add_scatter(slot, buf, batches, lanes):
        groups = {s: [] for s in subs}
        for batch, batch_lanes in zip(batches, lanes):
            s = batch[0]
            groups[s].append(plan.add(batch_lanes, result(slot, buf, s, groups[s])))
        return groups[0] + groups[1]

    partial_rowsplit(part, xf2, all_rows, dzf, all_rows)
    plan.work(3)
    scatter_3 = add_scatter(PAIR, part, BACK, scatter_lanes(part, 0, BACK, send_w_all, recv_c, give=True))
    product(backward_rowsplit, dzf, wg3, both, layer_emit(u2, 1, 0, PAIR), at_once)
    total = stat_sum(0)
    affine_grads(total, 0)
    copies = []
    for v in subs:
        def put_du2(rsl, value):
            duf[core, rsl, :] = value
        layer_rows(u2, 1, PAIR, total, v, put_du2)
        copies.append(share(duf, v))
    plan.work(1)
    plan.pump(plan.now + PAIR)
    for copy in q2:
        copy.wait_recv()
    product(backward_colsplit, duf, wg2, wq2, layer_emit(u1, 0, 1, 0), received(copies))
    sent(copies)
    scatter_2 = []

    def part2_lane(hh):
        yield NOW, {}, 1.9
        partial_colsplit(part2, xf1, duf, hh)
        plan.work(1.9)

    def start_2():
        scatter_2.extend(add_scatter(1, part2, BACK, scatter_lanes(part2, 1, BACK, send_g, recv_w_all, take=True)))

    part2_group = plan.add([part2_lane(hh) for hh in subs], start_2, first=True)
    total = stat_sum(1)
    plan.finish(part2_group)
    affine_grads(total, PAIR)
    dg_send, dg_recv = new_ids('s', 1)[0], new_ids('r', 1)[0]
    dg_copy = rcopy(dgb.at[core], dgb.at[core], dg_send, dg_recv, peer)
    dg_copy.start()

    for v in subs:
        def put_du1(rsl, value, v=v):
            start = rsl.start - v * vrows
            r = pl.multiple_of(lax.rem(start, rows), min(rstep, rows))
            c = lax.div(start, rows)
            for i in range(HALF_BLOCKS):
                du1[i // RING, i % RING, c, v, pl.ds(r, rstep), :] = value[:, i * blk:(i + 1) * blk]
        layer_rows(u1, 0, 0, total, v, put_du1)

    a2a_recv, a2a_send = new_ids('r', BLOCKS), new_ids('s', BLOCKS)
    targets = [(i // RING, i % RING, c) for i in range(HALF_BLOCKS) for c in subs]

    slots = (hx, zf, xf1, xf2)
    per = RING * rows

    turn = (0, 1, 3, PAIR)

    def h_fetch(chunk):
        at = chunk % RING
        begin = pl.multiple_of(near['z'][turn[chunk // PAIR]] * per, per)
        made = [pltpu.make_async_copy((h_a, h_b)[chunk % PAIR].at[pl.ds(begin, per), pl.ds(kh * half, half)],
                                      slots[at].at[kh], hsem.at[at * PAIR + kh]) for kh in subs]
        for copy in made:
            copy.start()
        return made

    fetches = [h_fetch(chunk) for chunk in range(RING)]
    own_half = lax.div(mid, HALF_BLOCKS)
    self_out = jnp.where(own_half == core, PAIR * (mid - HALF_BLOCKS * core) + core, -1)
    self_in = jnp.where(own_half == core, mid, -1)
    a2a_home, a2a_sem = a2a.at[zc, yc], rsem.at[a2a_recv[0] + mid]

    for k, (zi, yy, c) in enumerate(targets):
        src = du1.at[zi, yy, c]

        @pl.when(self_out == k)
        def _():
            a2a_home[...] = src[...]

        @pl.when(self_out != k)
        def _():
            pltpu.make_async_remote_copy(
                src_ref=src, dst_ref=a2a_home, send_sem=ssem.at[a2a_send[k]], recv_sem=a2a_sem,
                device_id=(HALF_BLOCKS * core + zi * RING + yy, x_base + c), device_id_type=MESH_ID).start()

    plan.work(1)
    arrived = max([plan.send(axis, 32 * rows * blk, TWO_HOPS) for axis in 'zy'])
    arrivals = [arrived - off for off in (4, PAIR, 1, 0)]
    for k in range(RING):
        plan.pump(arrivals[k])
        plan.until(arrivals[k])
        zz = near['z'][turn[k]]
        for i in range(RING):
            @pl.when(self_in != zz * RING + i)
            def _():
                pltpu.make_async_copy(a2a.at[zz, i], a2a.at[zz, i], rsem.at[a2a_recv[0] + zz * RING + i]).wait()
        for v in subs:
            chunk = PAIR * k + v
            at = chunk % RING
            for copy in fetches[chunk]:
                copy.wait()
            grad = jnp.concatenate([a2a[zz, i, v] for i in range(RING)], axis=0)
            for kh in subs:
                for q in range(RING):
                    res = dot_tn(grad, slots[at][kh, :, q * quad:(q + 1) * quad])
                    spot = (slice(kh * blk, (kh + 1) * blk), slice(q * quad, (q + 1) * quad))
                    u2[spot] = res + u2[spot] if chunk else res
            if chunk < RING:
                fetches.append(h_fetch(chunk + RING))
        plan.work(1)
    for k, (zi, yy, c) in enumerate(targets):
        @pl.when(self_out != k)
        def _():
            pltpu.make_async_copy(du1.at[zi, yy, c], du1.at[zi, yy, c], ssem.at[a2a_send[k]]).wait()

    x_recv, x_send = new_ids('r', RING), new_ids('s', RING)

    def strip(k, cols=pl.ds(0, half)):
        return u2.at[pl.ds(pl.multiple_of(k * blk, blk), blk), cols]

    swap = rcopy(strip(other), strip(PAIR), x_send[0], x_recv[0], peer)
    swap.start()
    plan.need['x'] = plan.now + 3.0
    plan.pump(plan.now + PAIR)
    swap.wait_recv()
    swap.wait_send()
    strip(core)[...] = strip(core)[...] + strip(PAIR)[...]
    shifts = [rcopy(strip(core, chunk_cols(near['x'][off])), strip(3, chunk_cols(off)), x_send[off], x_recv[off],
                    device('x', off)) for off in OTHERS]
    for copy in shifts:
        copy.start()
    arrived = plan.send('x', PAIR * quad * blk * RING, TWO_HOPS)
    plan.pump(arrived)
    for copy in shifts:
        copy.wait_recv()
    got = [strip(3, chunk_cols(off))[...] for off in OTHERS]
    piece_sum = (strip(core, chunk_cols(xc))[...] + got[0]) + (got[1] + got[2])
    for s in subs:
        out_w[0, core, xc, s] = piece_sum[:, s * blk:(s + 1) * blk].T
    sent(shifts)
    plan.need['x'] = FAR
    published.append(plan.add([publish(0, s) for s in subs], first=True))
    plan.finish(*scatter_3, *scatter_2)
    plan.finish(*published)
    dg_copy.wait_recv()
    dg_copy.wait_send()
    w_copy = pltpu.make_async_copy(out_w, dw_out, lsem.at[0])
    w_copy.start()
    small_out[...] = dgb[...]
    w_copy.wait()


def split_kernel(blk, dw_ref, small_ref, loss_out, dw1_out, dw2_out, dw3_out, dg1_out, db1_out, dg2_out, db2_out,
                 stage, sem_in, sem_out):
    half = HALF_BLOCKS * blk
    mid = lax.axis_index('model')
    loads = []
    for slot in range(3):
        loads.append(pltpu.make_async_copy(dw_ref.at[slot], stage.at[slot], sem_in.at[slot]))
        loads[-1].start()
    loss_out[...] = small_ref[0, FIRST:SECOND, half:half + 1] + small_ref[1, FIRST:SECOND, half:half + 1]
    for hh in range(PAIR):
        dg2_out[:, hh * half:(hh + 1) * half] = small_ref[hh, FIRST:SECOND, :half]
        db2_out[:, hh * half:(hh + 1) * half] = small_ref[hh, SECOND:PAIR, :half]
    mcols = pl.ds(pl.multiple_of(lax.rem(mid, HALF_BLOCKS) * blk, blk), blk)
    dg1_out[...] = small_ref[lax.div(mid, HALF_BLOCKS), 2:3, mcols]
    db1_out[...] = small_ref[lax.div(mid, HALF_BLOCKS), 3:4, mcols]
    stores = []
    for slot in range(3):
        loads[slot].wait()
        for t in range(BLOCKS):
            begin = pl.ds(t * blk, blk)
            dst = (dw1_out.at[begin, :], dw2_out.at[:, begin], dw3_out.at[begin, :])[slot]
            stores.append(pltpu.make_async_copy(stage.at[slot, t // HALF_BLOCKS, (t // PAIR) % RING, t % PAIR], dst,
                                                sem_out.at[len(stores)]))
            stores[-1].start()
    for copy in stores:
        copy.wait()


def build_call(blk, rows, total_rows, vmem_limit):
    dim, half = BLOCKS * blk, HALF_BLOCKS * blk
    trows = RING * rows
    pieces = (RING, RING, RING, PAIR, blk, blk)
    got = (PAIR, RING, RING, PAIR, blk, blk)
    act = pltpu.VMEM((PAIR, trows, half), BF16)
    pre = pltpu.VMEM((trows, half), F32)
    bank = (PAIR, RING, PAIR, blk, blk)
    dma = pltpu.SemaphoreType.DMA
    scratch = [
        act, pre, pre, pre, act, act, act,
        pltpu.VMEM(pieces, BF16), pltpu.VMEM(got, BF16), pltpu.VMEM(pieces, BF16), pltpu.VMEM(got, BF16),
        pltpu.VMEM(pieces, BF16),
        pltpu.VMEM(pieces, F32), pltpu.VMEM(pieces, F32),
        pltpu.VMEM((PAIR, 6, RING, PAIR, blk, blk), F32), pltpu.VMEM((PAIR, PAIR, 6, PAIR, blk, blk), F32),
        pltpu.VMEM((PAIR, PAIR, 3, blk, blk), F32),
        pltpu.VMEM((RING, RING, HALF_BLOCKS, blk), F32),
        pltpu.VMEM((PAIR, 3, RING, RING, half), F32), pltpu.VMEM((RING, RING, half), F32),
        pltpu.VMEM((PAIR, RING, half + blk), F32),
        pltpu.VMEM((PAIR, RING, half), F32), pltpu.VMEM((RING, RING, HALF_BLOCKS, blk), F32),
        pltpu.VMEM((RING, 40, blk), F32), pltpu.VMEM((PAIR, 40, blk), F32),
        pltpu.VMEM((PAIR, RING, PAIR, PAIR, rows, blk), BF16), pltpu.VMEM((RING, RING, PAIR, rows, blk), BF16),
        pltpu.VMEM((3,) + bank, F32),
        dma((N_SEND,)), dma((N_RECV,)), dma((BLOCKS,)), dma((HALF_BLOCKS,)), pltpu.SemaphoreType.REGULAR((12,)),
    ]
    anyspec = pl.BlockSpec(memory_space=pl.ANY)
    vmem = pl.BlockSpec(memory_space=pltpu.VMEM)
    smem = pl.BlockSpec(memory_space=pltpu.SMEM)
    packed = jax.ShapeDtypeStruct((3,) + bank, F32)
    step_call = pl.pallas_call(
        functools.partial(mega_kernel, (blk, rows, total_rows)),
        out_shape=[packed, jax.ShapeDtypeStruct((PAIR, RING, half + blk), F32)],
        in_specs=[anyspec] * 7 + [vmem, vmem, smem],
        out_specs=[anyspec, vmem],
        scratch_shapes=scratch,
        compiler_params=pltpu.CompilerParams(collective_id=0, has_side_effects=True, vmem_limit_bytes=vmem_limit),
        name='barlow_step',
    )

    def line(n):
        return jax.ShapeDtypeStruct((1, n), F32)

    tall, wide = jax.ShapeDtypeStruct((dim, blk), F32), jax.ShapeDtypeStruct((blk, dim), F32)
    split_call = pl.pallas_call(
        functools.partial(split_kernel, blk),
        out_shape=[line(1), tall, wide, tall, line(blk), line(blk), line(dim), line(dim)],
        in_specs=[anyspec, vmem],
        out_specs=[vmem, anyspec, anyspec, anyspec, vmem, vmem, vmem, vmem],
        scratch_shapes=[pltpu.VMEM((3,) + bank, F32), dma((3,)), dma((48,))],
        name='split_results',
    )

    def call(*args):
        return split_call(*step_call(*args))

    return call


def solution(mesh):
    data_size = mesh.shape['data']

    def shard_body(h_a, h_b, w_one, w_two, w_three, g_one, b_one, g_two, b_two, lam_off):
        group_rows = h_a.shape[0]
        blk = w_three.shape[1]
        rows = group_rows // BLOCKS
        call = build_call(blk, rows, group_rows * data_size, 67_000_000)
        outs = call(h_a, h_b, w_one, w_two, w_three, g_one.reshape(1, -1), b_one.reshape(1, -1),
                    g_two.reshape(1, -1), b_two.reshape(1, -1), lam_off)
        loss, dw1, dw2, dw3, dg1, db1, dg2, db2 = outs
        return (loss.reshape(1), dw1, dw2, dw3, dg1.reshape(-1), db1.reshape(-1), dg2.reshape(-1), db2.reshape(-1))

    in_specs = (P('data', None), P('data', None), P(None, 'model'), P('model', None), P(None, 'model'),
                P('model'), P('model'), P(), P(), P())
    out_specs = (P(), P(None, 'model'), P('model', None), P(None, 'model'), P('model'), P('model'), P(), P())
    return jax.shard_map(shard_body, mesh=mesh, in_specs=in_specs, out_specs=out_specs, check_vma=False)
```

time: 317 us -> 301 us (0.950)
  Pallas kernels: 316 us -> 300 us
    pallas_call x2, Pallas kernels: 316 us -> 300 us  [call(): return split_call(*step_call(*args))]
where the time goes in v3:
time: 301 us
  Pallas kernels  300 us (100%)
    pallas_call x2, Pallas kernels, call(): return split_call(*step_call(*args))  300 us

profile of v3, /device:TPU:1, one launch (start us, length us, event | category | flops | bytes accessed | tf_op | source)
XLA Modules:
  0.0 301.2 jit_solution(892978108924689332)
XLA Ops:
  1.3 295.1 %barlow_step.1 = (f32[3,2,4,2,128,128]{5,4,3,2,1,0:T(8,128)}, f32[2,4,1152]{2,1,0:T(4,128)}) custom-call(bf16[2048,2048]{1,0:T(8,128)(2,1)} %h_a.1, bf16[2048,2048]{1,0:T(8,128)(2,1)} %h_b.1, bf16[2048,128]{1,0:T(8,128)(2,1)} %w_one.1, bf16[128,2048]{1,0:T(8,128)(2,1)} %w_two.1, bf16[2048,128]{1,0:T(8,128)(2,1)} %w_three.1, f32[1,128]{1,0:T(1,128)} %bitcast.11, ...), custom_call_target="tpu_custom_call" | custom-call | tf_op jit(solution)/shard_map/barlow_step/pallas_call | solution.py:1097
  296.4 4.7 %split_results.1 = (f32[1,1]{1,0:T(1,128)}, f32[2048,128]{1,0:T(8,128)}, f32[128,2048]{1,0:T(8,128)}, f32[2048,128]{1,0:T(8,128)}, f32[1,128]{1,0:T(1,128)}, /*i...) custom-call(f32[3,2,4,2,128,128]{5,4,3,2,1,0:T(8,128)} %get-tuple-element.18.dw_ref, ...), custom_call_target="tpu_custom_call" | custom-call | tf_op jit(solution)/shard_map/split_results/pallas_call | solution.py:1097

commit v4 on v3

--- a/solution.py
+++ b/solution.py
@@ -15,7 +15,6 @@
 ORDERS = (('x', 'y', 'z'), ('y', 'z', 'x'), ('z', 'x', 'y'))
 COARSE = ((0, 0, (40, 48, 40)), (1, 0, (48, 40, 40)))
 FINE = COARSE
-MERGED = ((slice(PAIR), 0, (40, 48, 40)),)
 BACK = COARSE
 OTHERS = (1, 2, 3)
 N_SEND = 520
@@ -160,7 +159,31 @@
     peer = (mid, x_base + other)
 
     def device(axis, off):
-        return targets_of[axis][off]
+        if isinstance(off, int):
+            return targets_of[axis][off]
+        q = wrap(coord[axis] + off)
+        return {'z': (q * RING + yc, did), 'y': (z_base + q, did), 'x': (mid, q * PAIR + core)}[axis]
+
+    class Fan:
+        def __init__(self, axis, place, sid, rid):
+            def make(off):
+                src, dst = place(off)
+                return rcopy(src, dst, sid[0] + off - 1, rid[0] + off - 1, device(axis, off))
+            self.make = make
+
+        def each(self, action):
+            @pl.loop(1, RING)
+            def _(off):
+                getattr(self.make(off), action)()
+
+        def start(self):
+            self.each('start')
+
+        def wait_recv(self):
+            self.each('wait_recv')
+
+        def wait_send(self):
+            self.each('wait_send')
 
     z_own, z_other = PAIR * core, PAIR * other
     counters = {'s': 0, 'r': 0, 'l': 0}
@@ -178,7 +201,7 @@
     def bands(batches):
         for sub, begin, sizes in batches:
             for colour, size in enumerate(sizes):
-                yield sub, colour, pl.ds(begin, size), size * blk * (PAIR if isinstance(sub, slice) else 1)
+                yield sub, colour, pl.ds(begin, size), size * blk
                 begin += size
 
     def gather_lane(buf, sub, colour, rsl, cells, sid, rid):
@@ -197,15 +220,14 @@
         axis = order[0]
         yield NOW, {axis: PAIR * size}, NOW
         own = region(axis, (), coord[axis])
-        pending = [rcopy(own, own, sid[off - 1], rid[off - 1], device(axis, off)) for off in OTHERS]
-        for copy in pending:
-            copy.start()
+        pending = [Fan(axis, lambda off, own=own: (own, own), sid, rid)]
+        pending[0].start()
         ready = plan.send(axis, PAIR * size, TWO_HOPS)
         for phase in (1, 2):
             size *= RING
             axis, have = order[phase], order[:phase]
             yield ready, {axis: size}, STEP
-            for copy in pending[-3:] if phase == 1 else pending[-2:]:
+            for copy in pending[-PAIR:]:
                 copy.wait_recv()
             base = phase * RING - 1
             up, down = device(axis, 1), device(axis, 3)
@@ -340,14 +362,14 @@
         yield ready, {axis: size}, STEP
         finals()
         base = 12
-        last = []
-        for k, off in enumerate(OTHERS):
+
+        def spot(off):
             idx = dict(coord)
-            idx[axis] = near[axis][off]
-            last.append(rcopy(buf.at[idx['z'], idx['y'], idx['x'], sub, rsl, :], rv3.at[bank, sub, k, rsl, :],
-                              sid[base + k], rid[base + k], device(axis, off)))
-        for copy in last:
-            copy.start()
+            idx[axis] = wrap(coord[axis] + off)
+            return buf.at[idx['z'], idx['y'], idx['x'], sub, rsl, :], rv3.at[bank, sub, off - 1, rsl, :]
+
+        last = [Fan(axis, spot, sid[base:], rid[base:])]
+        last[0].start()
         yield plan.send(axis, size, TWO_HOPS), {}, STEP
         for copy in last:
             copy.wait_recv()
@@ -386,11 +408,8 @@
             if d:
                 stat[parity, d, coord[axis], :, width] = gathered_stat(parity, d - 1, pending)
             own = stat.at[parity, d, coord[axis], :, width]
-            copies = [rcopy(own, own, stat_send[d * 3 + off - 1], stat_recv[parity][d * 3 + off - 1], device(axis, off))
-                      for off in OTHERS]
-            for copy in copies:
-                copy.start()
-            pending.extend(copies)
+            pending.append(Fan(axis, lambda off, own=own: (own, own), stat_send[d * 3:], stat_recv[parity][d * 3:]))
+            pending[-1].start()
             ready = plan.send(axis, STAT_SIZE, TWO_HOPS)
         yield ready, {}, STEP
         out.append(gathered_stat(parity, d, pending))
@@ -398,8 +417,7 @@
             copy.wait_send()
 
     def gathered_stat(parity, d, pending):
-        for copy in pending[-3:]:
-            copy.wait_recv()
+        pending[-1].wait_recv()
         got = [stat[parity, d, q, :, :half] for q in range(RING)]
         return (got[0] + got[1]) + (got[PAIR] + got[3])
 
@@ -478,9 +496,8 @@
             yield ready, {axis: STAT_SIZE}, NOW
             for copy in sent_copies:
                 copy.wait_recv()
-            made = [rcopy(own, own, stat_send[k + off - 1], gb_recv[k + off - 1], device(axis, off)) for off in OTHERS]
-            for copy in made:
-                copy.start()
+            made = [Fan(axis, lambda off, own=own: (own, own), stat_send[k:], gb_recv[k:])]
+            made[0].start()
             ready = plan.send(axis, STAT_SIZE, TWO_HOPS)
             sent_copies.extend(made)
         yield ready, {}, NOW
@@ -499,9 +516,9 @@
     for copy in more_loads:
         copy.wait()
     gather1.append(plan.add([gain_lane()], first=True))
-    gather2 = add_gather(wg2, wq2, MERGED, send_w[1], recv_w[1], PAIR, q2)
+    gather2 = add_gather(wg2, wq2, COARSE, send_w[1], recv_w[1], PAIR, q2)
     plan.finish(*gather1, alone=True)
-    gather3 = add_gather(wg3, wq1, MERGED, send_w[PAIR], recv_w[PAIR], RING, q3, held3)
+    gather3 = add_gather(wg3, wq1, COARSE, send_w[PAIR], recv_w[PAIR], RING, q3, held3)
     for copy in h_copies:
         copy.wait_recv()
     plan.pump(plan.now + STEP)
@@ -744,17 +761,15 @@
         ready, pending = NOW, []
         for k, axis in enumerate(AXES[::-1][1:] + AXES[PAIR:]):
             yield ready, {axis: STAT_SIZE}, STEP
-            for copy in pending[-3:]:
+            for copy in pending[-1:]:
                 copy.wait_recv()
             if axis == 'x':
                 plane = [vec[t // RING, t % RING] for t in range(BLOCKS)]
                 rest_rows = sum(plane[1:], plane[0])
                 vecx[xc] = jnp.concatenate([item[:PAIR] for item in plane] + [rest_rows], axis=0)
             own = {'y': vec.at[zc, yc], 'z': vec.at[zc], 'x': vecx.at[xc]}[axis]
-            made = [rcopy(own, own, vec_send[k * 3 + off - 1], vec_recv[k * 3 + off - 1], device(axis, off))
-                    for off in OTHERS]
-            for copy in made:
-                copy.start()
+            made = [Fan(axis, lambda off, own=own: (own, own), vec_send[k * 3:], vec_recv[k * 3:])]
+            made[0].start()
             ready = plan.send(axis, STAT_SIZE, TWO_HOPS)
             pending.extend(made)
         yield ready, {}, STEP
@@ -911,7 +926,6 @@
         layer_rows(u1, 0, 0, total, v, put_du1)
 
     a2a_recv, a2a_send = new_ids('r', BLOCKS), new_ids('s', BLOCKS)
-    targets = [(i // RING, i % RING, c) for i in range(HALF_BLOCKS) for c in subs]
 
     slots = (hx, zf, xf1, xf2)
     per = RING * rows
@@ -933,18 +947,21 @@
     self_in = jnp.where(own_half == core, mid, -1)
     a2a_home, a2a_sem = a2a.at[zc, yc], rsem.at[a2a_recv[0] + mid]
 
-    for k, (zi, yy, c) in enumerate(targets):
-        src = du1.at[zi, yy, c]
-
+    def block(k):
+        return du1.at[lax.div(k, HALF_BLOCKS), wrap(lax.div(k, PAIR)), lax.rem(k, PAIR)]
+
+    @pl.loop(0, BLOCKS)
+    def _(k):
         @pl.when(self_out == k)
         def _():
-            a2a_home[...] = src[...]
+            a2a_home[...] = block(k)[...]
 
         @pl.when(self_out != k)
         def _():
             pltpu.make_async_remote_copy(
-                src_ref=src, dst_ref=a2a_home, send_sem=ssem.at[a2a_send[k]], recv_sem=a2a_sem,
-                device_id=(HALF_BLOCKS * core + zi * RING + yy, x_base + c), device_id_type=MESH_ID).start()
+                src_ref=block(k), dst_ref=a2a_home, send_sem=ssem.at[a2a_send[0] + k], recv_sem=a2a_sem,
+                device_id=(HALF_BLOCKS * core + lax.div(k, PAIR), x_base + lax.rem(k, PAIR)),
+                device_id_type=MESH_ID).start()
 
     plan.work(1)
     arrived = max([plan.send(axis, 32 * rows * blk, TWO_HOPS) for axis in 'zy'])
@@ -953,7 +970,8 @@
         plan.pump(arrivals[k])
         plan.until(arrivals[k])
         zz = near['z'][turn[k]]
-        for i in range(RING):
+        @pl.loop(0, RING)
+        def _(i):
             @pl.when(self_in != zz * RING + i)
             def _():
                 pltpu.make_async_copy(a2a.at[zz, i], a2a.at[zz, i], rsem.at[a2a_recv[0] + zz * RING + i]).wait()
@@ -971,10 +989,11 @@
             if chunk < RING:
                 fetches.append(h_fetch(chunk + RING))
         plan.work(1)
-    for k, (zi, yy, c) in enumerate(targets):
+    @pl.loop(0, BLOCKS)
+    def _(k):
         @pl.when(self_out != k)
         def _():
-            pltpu.make_async_copy(du1.at[zi, yy, c], du1.at[zi, yy, c], ssem.at[a2a_send[k]]).wait()
+            pltpu.make_async_copy(block(k), block(k), ssem.at[a2a_send[0] + k]).wait()
 
     x_recv, x_send = new_ids('r', RING), new_ids('s', RING)
 
@@ -988,8 +1007,8 @@
     swap.wait_recv()
     swap.wait_send()
     strip(core)[...] = strip(core)[...] + strip(PAIR)[...]
-    shifts = [rcopy(strip(core, chunk_cols(near['x'][off])), strip(3, chunk_cols(off)), x_send[off], x_recv[off],
-                    device('x', off)) for off in OTHERS]
+    shifts = [Fan('x', lambda off: (strip(core, chunk_cols(wrap(xc + off))), strip(3, chunk_cols(off))), x_send[1:],
+                  x_recv[1:])]
     for copy in shifts:
         copy.start()
     arrived = plan.send('x', PAIR * quad * blk * RING, TWO_HOPS)

time: 301 us -> 296 us (0.983)
  Pallas kernels: 300 us -> 294 us
    pallas_call x2, Pallas kernels: 300 us -> 294 us  [call(): return split_call(*step_call(*args))]
where the time goes in v4:
time: 296 us; the launch traced here: 295 us
  Pallas kernels  294 us (99%)
    pallas_call x2, Pallas kernels, call(): return split_call(*step_call(*args))  294 us

profile of v4, /device:TPU:1, one launch (start us, length us, event | category | flops | bytes accessed | tf_op | source)
XLA Modules:
  0.0 295.3 jit_solution(16983599583704866122)
XLA Ops:
  1.3 289.2 %barlow_step.1 = (f32[3,2,4,2,128,128]{5,4,3,2,1,0:T(8,128)}, f32[2,4,1152]{2,1,0:T(4,128)}) custom-call(bf16[2048,2048]{1,0:T(8,128)(2,1)} %h_a.1, bf16[2048,2048]{1,0:T(8,128)(2,1)} %h_b.1, bf16[2048,128]{1,0:T(8,128)(2,1)} %w_one.1, bf16[128,2048]{1,0:T(8,128)(2,1)} %w_two.1, bf16[2048,128]{1,0:T(8,128)(2,1)} %w_three.1, f32[1,128]{1,0:T(1,128)} %bitcast.11, ...), custom_call_target="tpu_custom_call" | custom-call | tf_op jit(solution)/shard_map/barlow_step/pallas_call | solution.py:1116
  290.5 4.7 %split_results.1 = (f32[1,1]{1,0:T(1,128)}, f32[2048,128]{1,0:T(8,128)}, f32[128,2048]{1,0:T(8,128)}, f32[2048,128]{1,0:T(8,128)}, f32[1,128]{1,0:T(1,128)}, /*i...) custom-call(f32[3,2,4,2,128,128]{5,4,3,2,1,0:T(8,128)} %get-tuple-element.18.dw_ref, ...), custom_call_target="tpu_custom_call" | custom-call | tf_op jit(solution)/shard_map/split_results/pallas_call | solution.py:1116

commit v5 on v4

--- a/solution.py
+++ b/solution.py
@@ -17,8 +17,8 @@
 FINE = COARSE
 BACK = COARSE
 OTHERS = (1, 2, 3)
-N_SEND = 520
-N_RECV = 520
+N_SEND = 560
+N_RECV = 560
 BYTES_PER_US = 46600.0
 HOP = 1.9
 TWO_HOPS = 2.7
@@ -63,7 +63,7 @@
     def __init__(self):
         self.now = 0.0
         self.free = dict.fromkeys(AXES, 0.0)
-        self.need = dict.fromkeys(AXES, FAR)
+        self.need = [dict.fromkeys(AXES, FAR) for _ in range(PAIR)]
         self.lanes = []
         self.first = None
 
@@ -78,7 +78,7 @@
         return self.free[axis] + flight
 
     def add(self, gens, then=None, first=False):
-        group = {'left': 0, 'then': then}
+        group = {'left': 0, 'then': then, 'done': NOW, 'first': first}
         made = []
         for gen in gens:
             group['left'] += 1
@@ -91,10 +91,12 @@
         start = max(self.now, ready() if callable(ready) else ready)
         if self.first is not None and lane[2] not in self.first and max(loads.values(), default=0) > SMALL:
             return FAR
+        if not lane[2]['first']:
+            for axis in loads:
+                start = max(start, self.free[axis] - BACKLOG)
         for axis, size in loads.items():
-            start = max(start, self.free[axis] - BACKLOG)
-        for axis, size in loads.items():
-            if max(self.free[axis], start) + size / BYTES_PER_US > self.need[axis] + 1.0:
+            needed = min(need[axis] for need in self.need)
+            if not lane[2]['first'] and max(self.free[axis], start) + size / BYTES_PER_US > needed + 1.0:
                 return FAR
         return start
 
@@ -114,6 +116,7 @@
         self.lanes = [lane for lane in self.lanes if lane is not best]
         group = best[2]
         group['left'] -= 1
+        group['done'] = self.now
         if not group['left'] and group['then'] is not None:
             group['then']()
         return True
@@ -126,19 +129,25 @@
         self.first = groups if alone else None
         while any(group['left'] for group in groups):
             if not self.advance(FAR):
-                self.need = dict.fromkeys(AXES, FAR)
+                self.clear()
         self.first = None
 
-    def expect(self, when):
+    def clear(self):
+        for need in self.need:
+            need.update(dict.fromkeys(AXES, FAR))
+
+    def expect(self, v, when, axes=AXES):
         for axis in AXES:
-            self.need[axis] = when
+            self.need[v][axis] = FAR
+        for axis in axes:
+            self.need[v][axis] = when
             when += 3.6
 
 
 def mega_kernel(cfg, h_a, h_b, w_one, w_two, w_three, g_one, b_one, g_two, b_two, lam_ref,
-                dw_out, small_out,
+                out_w, small_out,
                 hx, u1, u2, u3, xf1, xf2, zf, wg1, wq1, wg2, wq2, wg3, part, part2, rv1, rv2, rv3,
-                gbuf, stat, sres, dgb, zsum, vec, vecx, vecp, du1, a2a, out_w, ssem, rsem, lsem, hsem, credit):
+                gbuf, stat, sres, dgb, zsum, vec, vecx, vecp, du1, a2a, ssem, rsem, lsem, hsem, credit):
     blk, rows, total_rows = cfg
     plan = Plan()
     half = HALF_BLOCKS * blk
@@ -398,42 +407,30 @@
             made.append(copy)
         return send
 
-    stat_recv = [new_ids('r', 9) for _ in range(PAIR)]
-    stat_send = new_ids('s', 9)
-
-    def stat_steps(parity, out):
-        pending, ready, width = [], NOW, slice(half)
+    stat_recv = [[new_ids('r', 9) for _ in range(PAIR)] for _ in range(PAIR)]
+    stat_send = [new_ids('s', 9) for _ in range(PAIR)]
+
+    def stat_steps(parity, v, out):
+        pending, ready = [], plan.now
         for d, axis in enumerate(AXES):
-            yield ready, {axis: STAT_SIZE}, STEP
+            plan.expect(v, ready, AXES[d:])
+            yield ready, {axis: STAT_SIZE / PAIR}, STEP
             if d:
-                stat[parity, d, coord[axis], :, width] = gathered_stat(parity, d - 1, pending)
-            own = stat.at[parity, d, coord[axis], :, width]
-            pending.append(Fan(axis, lambda off, own=own: (own, own), stat_send[d * 3:], stat_recv[parity][d * 3:]))
+                stat[parity, v, d, coord[axis]] = gathered_stat(parity, v, d - 1, pending)
+            own = stat.at[parity, v, d, coord[axis]]
+            pending.append(Fan(axis, lambda off, own=own: (own, own), stat_send[v][d * 3:], stat_recv[parity][v][d * 3:]))
             pending[-1].start()
-            ready = plan.send(axis, STAT_SIZE, TWO_HOPS)
+            ready = plan.send(axis, STAT_SIZE / PAIR, TWO_HOPS + 0.5)
+        plan.expect(v, FAR)
         yield ready, {}, STEP
-        out.append(gathered_stat(parity, d, pending))
+        out.append(gathered_stat(parity, v, d, pending))
         for copy in pending:
             copy.wait_send()
 
-    def gathered_stat(parity, d, pending):
+    def gathered_stat(parity, v, d, pending):
         pending[-1].wait_recv()
-        got = [stat[parity, d, q, :, :half] for q in range(RING)]
+        got = [stat[parity, v, d, q] for q in range(RING)]
         return (got[0] + got[1]) + (got[PAIR] + got[3])
-
-    def stat_sum(parity):
-        out = []
-        steps = stat_steps(parity, out)
-        next(steps)
-        plan.expect(plan.now)
-        for axis in AXES:
-            ready = next(steps)[0]
-            plan.need[axis] = FAR
-            plan.pump(ready)
-            plan.until(ready)
-            plan.work(STEP)
-        next(steps, None)
-        return out[0]
 
     def row(k):
         return slice(k, k + 1)
@@ -445,8 +442,8 @@
         return row(PAIR * v + 1)
 
     def put_stat(parity, v, cols, first, second):
-        stat[parity, 0, zc, first_row(v), cols] = first
-        stat[parity, 0, zc, second_row(v), cols] = second
+        stat[parity, v, 0, zc, row(FIRST), cols] = first
+        stat[parity, v, 0, zc, row(SECOND), cols] = second
 
     def local(src, dst):
         copy = pltpu.make_async_copy(src, dst, lsem.at[new_ids('l', 1)[0]])
@@ -496,7 +493,7 @@
             yield ready, {axis: STAT_SIZE}, NOW
             for copy in sent_copies:
                 copy.wait_recv()
-            made = [Fan(axis, lambda off, own=own: (own, own), stat_send[k:], gb_recv[k:])]
+            made = [Fan(axis, lambda off, own=own: (own, own), stat_send[0][k:], gb_recv[k:])]
             made[0].start()
             ready = plan.send(axis, STAT_SIZE, TWO_HOPS)
             sent_copies.extend(made)
@@ -519,21 +516,10 @@
     gather2 = add_gather(wg2, wq2, COARSE, send_w[1], recv_w[1], PAIR, q2)
     plan.finish(*gather1, alone=True)
     gather3 = add_gather(wg3, wq1, COARSE, send_w[PAIR], recv_w[PAIR], RING, q3, held3)
-    for copy in h_copies:
-        copy.wait_recv()
-    plan.pump(plan.now + STEP)
-    for copy in q1:
-        copy.wait_recv()
-    plan.work(PAIR)
-
     def gathered(k):
         return lanes_of(gbuf[z, i, row(k), :] for z in (z_own, z_own + 1) for i in range(RING))
 
-    gain1, shift1 = gathered(0), gathered(1)
     my_cols = pl.ds(pl.multiple_of(core * half, half), half)
-    gain2, shift2 = g_two[:, my_cols], b_two[:, my_cols]
-    for k, value in enumerate((gain1, shift1, gain2, shift2)):
-        sres[3, row(k), :] = value
 
     def view_rows(v):
         return pl.ds(v * vrows, vrows)
@@ -544,9 +530,8 @@
     def over_chunks(fn):
         pl.loop(0, RING)(fn)
 
-    def forward_rowsplit(act, own, got, views, emit, ready):
+    def forward_rowsplit(act, own, got, views, emit):
         for v, src_v in views:
-            ready[v]()
 
             def body(j):
                 zz, y0 = lax.div(j, PAIR), lax.rem(j, PAIR) * PAIR
@@ -556,9 +541,8 @@
                      + dot_nn(act[other, view_rows(src_v), :], sides[1]))
             over_chunks(body)
 
-    def forward_colsplit(act, own, emit, ready):
-        for v in subs:
-            ready[v]()
+    def forward_colsplit(act, own, views, emit):
+        for v, _ in views:
 
             def body(j):
                 sides = [lanes_of(own[PAIR * hh:PAIR * hh + PAIR, :, j, s].reshape(half, blk) for s in subs)
@@ -566,9 +550,8 @@
                 emit(j, v, dot_nn(act[0, view_rows(v), :], sides[0]) + dot_nn(act[1, view_rows(v), :], sides[1]))
             over_chunks(body)
 
-    def backward_rowsplit(act, own, views, emit, ready):
+    def backward_rowsplit(act, own, views, emit):
         for v, src_v in views:
-            ready[v]()
 
             def body(j):
                 sides = [lanes_of(own[PAIR * hh + i // RING, i % RING, j].reshape(quad, blk) for i in range(HALF_BLOCKS))
@@ -577,9 +560,8 @@
                      + dot_nt(act[1, view_rows(src_v), :], sides[1]))
             over_chunks(body)
 
-    def backward_colsplit(act, own, got, emit, ready):
-        for v in subs:
-            ready[v]()
+    def backward_colsplit(act, own, got, views, emit):
+        for v, _ in views:
 
             def body(j):
                 sides = []
@@ -620,12 +602,11 @@
             put_stat(parity, v, cols, col_sum(acc), col_sum(acc * acc))
         return emit
 
-    def moments(total, slot):
-        for v in subs:
-            mean = total[first_row(v), :half] * inv_n
-            inv = lax.rsqrt(total[second_row(v), :half] * inv_n - mean * mean + BN_EPS)
-            sres[slot, first_row(v), :] = mean
-            sres[slot, second_row(v), :] = inv
+    def moments(total, slot, v):
+        mean = total[row(FIRST)] * inv_n
+        inv = lax.rsqrt(total[row(SECOND)] * inv_n - mean * mean + BN_EPS)
+        sres[slot, first_row(v), :] = mean
+        sres[slot, second_row(v), :] = inv
 
     act_send, act_recv = new_ids('s', PAIR), new_ids('r', 10)
 
@@ -642,83 +623,118 @@
         def _(i):
             fn(pl.ds(pl.multiple_of(v * vrows + i * rstep, rstep), rstep))
 
-    def activate(src, slot, gain, shift, dst):
-        copies = []
-        for v in subs:
-            mean = sres[slot, first_row(v), :]
-            inv = sres[slot, second_row(v), :]
-
-            def fn(rsl, mean=mean, inv=inv):
-                norm = (src[rsl, :] - mean) * inv
-                if gain is not None:
-                    norm = jnp.maximum(gain * norm + shift, NOW)
-                dst[core, rsl, :] = norm.astype(BF16)
-            apply_rows(v, fn)
-            copies.append(share(dst, v))
-        plan.work(1)
-        plan.pump(plan.now + PAIR)
-        return copies
-
-    def received(copies):
-        return [copy.wait_recv for copy in copies]
+    def activate(src, slot, v, gain, shift, dst):
+        mean = sres[slot, first_row(v), :]
+        inv = sres[slot, second_row(v), :]
+
+        def fn(rsl):
+            norm = (src[rsl, :] - mean) * inv
+            if gain is not None:
+                norm = jnp.maximum(gain[...] * norm + shift[...], NOW)
+            dst[core, rsl, :] = norm.astype(BF16)
+        apply_rows(v, fn)
+        return share(dst, v)
+
+    def nothing():
+        pass
 
     def sent(copies):
         for copy in copies:
             copy.wait_send()
 
-    def nothing():
-        pass
-
-    both = ((0, 0), (1, 1))
-    at_once = (nothing, nothing)
     all_rows = pl.ds(0, PAIR * vrows)
-
-    MM = 3.7
-
-    def product(fn, *args):
-        plan.expect(plan.now + MM)
-        plan.pump(plan.now + STEP)
-        fn(*args)
+    MM = 1.85
+    SHARE = 2.2
+    occurred = set()
+
+    def once(name, fn):
+        if name not in occurred:
+            occurred.add(name)
+            fn()
+
+    def after(groups, extra=NOW):
+        def ready():
+            return FAR if any(group['left'] for group in groups) else max(group['done'] for group in groups) + extra
+        return ready
+
+    def at_last(*readies):
+        return lambda: max(ready() if callable(ready) else ready for ready in readies)
+
+    shares = {}
+
+    def dense(v, name, ready, before, product, src, slot, parity, gain, shift, dst):
+        plan.expect(v, FAR)
+        yield ready, {}, MM
+        before()
+        product(v)
         plan.work(MM)
-
-    product(forward_rowsplit, hx, wg1, wq1, both, forward_emit(u1, 0), at_once)
-    moments(stat_sum(0), 0)
-    copies = activate(u1, 0, gain1, shift1, xf1)
-    sent(q1 + h_copies)
-    plan.finish(*gather2)
-    product(forward_colsplit, xf1, wg2, forward_emit(u2, 1), received(copies))
-    released.append(True)
-    for send in held3:
-        send()
-    sent(copies)
-    moments(stat_sum(1), 1)
-    copies = activate(u2, 1, gain2, shift2, xf2)
-    plan.finish(*gather3)
-    for copy in q3:
+        out = []
+        yield from stat_steps(parity, v, out)
+        moments(out[0], slot, v)
+        copy = activate(src, slot, v, gain, shift, dst)
+        plan.work(0.5)
+        yield plan.now + SHARE, {}, NOW
         copy.wait_recv()
-    product(forward_rowsplit, xf2, wg3, wq1, both, forward_emit(u3, 0), received(copies))
-    sent(copies)
-    moments(stat_sum(0), PAIR)
-    copies = activate(u3, PAIR, None, None, zf)
-    for copy in copies:
-        copy.wait_recv()
-    sent(copies)
-
-    for v in subs:
-        stat[1, 0, zc, row(v), :half] = col_sum(zf[core, view_rows(v), :].astype(F32))
-    zsum_ids = new_ids('s', 1) + new_ids('r', 1)
-
-    def zsum_lane():
+        copy.wait_send()
+        shares[name, v] = True
+
+    zsum_ids = [new_ids('s', 1) + new_ids('r', 1) for _ in subs]
+
+    def settle_h():
+        for copy in h_copies:
+            copy.wait_recv()
+        for copy in h_copies:
+            copy.wait_send()
+        for copy in q1:
+            copy.wait_recv()
+        for copy in q1:
+            copy.wait_send()
+        gains = (gathered(FIRST), gathered(SECOND), g_two[:, my_cols], b_two[:, my_cols])
+        for k, value in enumerate(gains):
+            sres[3, row(k), :] = value
+
+    def release():
+        released.append(True)
+        for send in held3:
+            send()
+
+    def settle_q3():
+        for copy in q3:
+            copy.wait_recv()
+
+    def forward_lane(v):
+        views = ((v, v),)
+        yield from dense(v, 1, after(gather1, 3.0), lambda: once('h', settle_h),
+                         lambda v: forward_rowsplit(hx, wg1, wq1, views, forward_emit(u1, 0)), u1, 0, 0,
+                         sres.at[3, row(FIRST)], sres.at[3, row(SECOND)], xf1)
+        if (1, 1 - v) in shares:
+            release()
+        yield from dense(v, PAIR, after(gather2), nothing,
+                         lambda v: forward_colsplit(xf1, wg2, views, forward_emit(u2, 1)), u2, 1, 1,
+                         sres.at[3, row(PAIR)], sres.at[3, row(3)], xf2)
+        yield from dense(v, 3, lambda: after(gather3, 3.0)() if len(q3) == PAIR else FAR, lambda: once('q3', settle_q3),
+                         lambda v: forward_rowsplit(xf2, wg3, wq1, views, forward_emit(u3, 0)), u3, PAIR, 0,
+                         None, None, zf)
+        plan.add([zsum_lane(v)], summed, first=True)
+
+    def summed():
+        shares['sums', len(shares)] = True
+
+    def zsum_lane(v):
+        yield NOW, {}, STEP
+        stat[1, v, 0, zc, row(FIRST), :] = col_sum(zf[core, view_rows(v), :].astype(F32))
+        stat[1, v, 0, zc, row(SECOND), :] = jnp.zeros((1, half), F32)
         out = []
-        yield from stat_steps(1, out)
-        zsum[core] = out[0]
-        copy = rcopy(zsum.at[core], zsum.at[core], *zsum_ids, peer)
+        yield from stat_steps(1, v, out)
+        zsum[core, v] = out[0]
+        copy = rcopy(zsum.at[core, v], zsum.at[core, v], *zsum_ids[v], peer)
         copy.start()
         yield plan.now + PAIR, {}, NOW
         copy.wait_recv()
         copy.wait_send()
 
-    zsum_group = plan.add([zsum_lane()], first=True)
+    forward = plan.add([forward_lane(v) for v in subs], first=True)
+    plan.finish(forward)
 
     partial_rowsplit(part, zf, view_rows(0), zf, view_rows(1))
     lam = lam_ref[0]
@@ -742,14 +758,16 @@
     lanes_g = gather_lanes(wg1, FINE, send_g, recv_w_all)
     scatter_c = [plan.add(lanes, gradient_of(k, FINE[k]))
                  for k, lanes in enumerate(scatter_lanes(part, 0, FINE, send_w_all, recv_c))]
-    plan.finish(zsum_group, *scatter_c)
+    plan.finish(*scatter_c)
+    while sum(name == 'sums' for name, _ in shares) < PAIR:
+        plan.advance(FAR)
 
     share_of = []
-    sum_b = zsum[lax.div(mid, HALF_BLOCKS), row(SECOND), pl.ds(pl.multiple_of(lax.rem(mid, HALF_BLOCKS) * blk, blk), blk)]
+    sum_b = zsum[lax.div(mid, HALF_BLOCKS), SECOND, row(FIRST), pl.ds(pl.multiple_of(lax.rem(mid, HALF_BLOCKS) * blk, blk), blk)]
     for s in subs:
         grad = wg1[zc, yc, xc, s].astype(F32)
         both_terms = grad * (part[zc, yc, xc, s] * inv_n)
-        sum_a = zsum[core, row(FIRST), pl.ds(pl.multiple_of(xc * quad + s * blk, blk), blk)]
+        sum_a = zsum[core, FIRST, row(FIRST), pl.ds(pl.multiple_of(xc * quad + s * blk, blk), blk)]
         share_of.append((col_sum((grad.T * sum_a).T) * inv_n, col_sum(both_terms), col_sum((grad * sum_b).T) * inv_n,
                          col_sum(both_terms.T)))
     (c0, c1, r00, r10), (d0, d1, r01, r11) = share_of
@@ -784,34 +802,42 @@
         sent(pending + [copy])
 
     vec_group = plan.add([vec_lane()], first=True)
-    plan.finish(*gather_g)
+
+    dzf, duf = hx, zf
 
     def embed_emit(j, v, acc):
         u3[view_rows(v), chunk_cols(j)] = acc * inv_n
 
-    backward_rowsplit(zf, wg1, ((0, 1),), embed_emit, at_once)
-    for copy in qg:
-        copy.wait_recv()
-    forward_rowsplit(zf, wg1, wq1, ((1, 0),), embed_emit, at_once)
-    dzf, duf = hx, zf
-    plan.work(MM)
-    plan.finish(vec_group)
-    first_r = PAIR * BLOCKS + PAIR
-    dgb[core, :, half:half + blk] = jnp.broadcast_to(vecp[core, row(first_r + RING), :], (RING, blk))
-    mine = pl.ds(pl.multiple_of(BLOCKS * core, BLOCKS), BLOCKS)
-    both_cores = vecp[0, mine, :] + vecp[1, mine, :]
-    sums = [[lanes_of(vecx[q, row(first_r + PAIR * t + s), :] for q in range(RING) for s in subs) for t in subs],
-            [lanes_of(both_cores[row(PAIR * i + t)] for i in range(HALF_BLOCKS)) for t in subs]]
-    copies = []
-    for v in subs:
-        def embed_rows(rsl, mean_g=sums[v][0], mean_gz=sums[v][1], inv=sres[PAIR, second_row(v), :]):
+    def settle_qg():
+        for copy in qg:
+            copy.wait_recv()
+
+    def embed_product(v):
+        if v:
+            once('qg', settle_qg)
+            forward_rowsplit(zf, wg1, wq1, ((1, 0),), embed_emit)
+        else:
+            backward_rowsplit(zf, wg1, ((0, 1),), embed_emit)
+
+    sums = []
+
+    def embed_sums():
+        first_r = PAIR * BLOCKS + PAIR
+        dgb[core, :, half:half + blk] = jnp.broadcast_to(vecp[core, row(first_r + RING), :], (RING, blk))
+        mine = pl.ds(pl.multiple_of(BLOCKS * core, BLOCKS), BLOCKS)
+        both_cores = vecp[0, mine, :] + vecp[1, mine, :]
+        sums.append([lanes_of(vecx[q, row(first_r + PAIR * t + s), :] for q in range(RING) for s in subs) for t in subs])
+        sums.append([lanes_of(both_cores[row(PAIR * i + t)] for i in range(HALF_BLOCKS)) for t in subs])
+
+    def embed_apply(v):
+        once('sums', embed_sums)
+        mean_g, mean_gz = sums[v]
+        inv = sres[PAIR, second_row(v), :]
+
+        def fn(rsl):
             emb = zf[core, rsl, :].astype(F32)
             dzf[core, rsl, :] = (inv * (u3[rsl, :] - (mean_g + emb * mean_gz) * inv_n)).astype(BF16)
-        apply_rows(v, embed_rows)
-        copies.append(share(dzf, v))
-    for copy in copies:
-        copy.wait_recv()
-    sent(copies + q2 + q3 + qg)
+        apply_rows(v, fn)
 
     out_ids = {(slot, s): (new_ids('s', 5), new_ids('r', 5)) for slot in range(3) for s in subs}
 
@@ -860,7 +886,7 @@
         return emit
 
     def layer_rows(src, slot, k, total, v, store):
-        sum_lin, sum_norm = total[first_row(v), :half], total[second_row(v), :half]
+        sum_lin, sum_norm = total[row(FIRST)], total[row(SECOND)]
         mean, inv = sres[slot, first_row(v), :], sres[slot, second_row(v), :]
         scale = sres[3, row(k), :] * inv
 
@@ -870,8 +896,12 @@
         apply_rows(v, fn)
 
     def affine_grads(total, k):
-        dgb[core, row(k), :half] = total[second_row(FIRST), :half] + total[second_row(SECOND), :half]
-        dgb[core, row(k + 1), :half] = total[first_row(FIRST), :half] + total[first_row(SECOND), :half]
+        spots = ((row(k), total[row(SECOND)]), (row(k + 1), total[row(FIRST)]))
+        for spot, value in spots:
+            if ('affine', k) in occurred:
+                value = value + dgb[core, spot, :half]
+            dgb[core, spot, :half] = value
+        occurred.add(('affine', k))
 
     def add_scatter(slot, buf, batches, lanes):
         groups = {s: [] for s in subs}
@@ -880,25 +910,15 @@
             groups[s].append(plan.add(batch_lanes, result(slot, buf, s, groups[s])))
         return groups[0] + groups[1]
 
-    partial_rowsplit(part, xf2, all_rows, dzf, all_rows)
-    plan.work(3)
-    scatter_3 = add_scatter(PAIR, part, BACK, scatter_lanes(part, 0, BACK, send_w_all, recv_c, give=True))
-    product(backward_rowsplit, dzf, wg3, both, layer_emit(u2, 1, 0, PAIR), at_once)
-    total = stat_sum(0)
-    affine_grads(total, 0)
-    copies = []
-    for v in subs:
-        def put_du2(rsl, value):
-            duf[core, rsl, :] = value
-        layer_rows(u2, 1, PAIR, total, v, put_du2)
-        copies.append(share(duf, v))
-    plan.work(1)
-    plan.pump(plan.now + PAIR)
-    for copy in q2:
-        copy.wait_recv()
-    product(backward_colsplit, duf, wg2, wq2, layer_emit(u1, 0, 1, 0), received(copies))
-    sent(copies)
-    scatter_2 = []
+    scatter_3, scatter_2, part2_groups = [], [], []
+
+    def part3_lane():
+        yield NOW, {}, 3.0
+        partial_rowsplit(part, xf2, all_rows, dzf, all_rows)
+        plan.work(3)
+
+    def start_3():
+        scatter_3.extend(add_scatter(PAIR, part, BACK, scatter_lanes(part, 0, BACK, send_w_all, recv_c, give=True)))
 
     def part2_lane(hh):
         yield NOW, {}, 1.9
@@ -908,92 +928,148 @@
     def start_2():
         scatter_2.extend(add_scatter(1, part2, BACK, scatter_lanes(part2, 1, BACK, send_g, recv_w_all, take=True)))
 
-    part2_group = plan.add([part2_lane(hh) for hh in subs], start_2, first=True)
-    total = stat_sum(1)
-    plan.finish(part2_group)
-    affine_grads(total, PAIR)
-    dg_send, dg_recv = new_ids('s', 1)[0], new_ids('r', 1)[0]
-    dg_copy = rcopy(dgb.at[core], dgb.at[core], dg_send, dg_recv, peer)
-    dg_copy.start()
-
-    for v in subs:
-        def put_du1(rsl, value, v=v):
-            start = rsl.start - v * vrows
-            r = pl.multiple_of(lax.rem(start, rows), min(rstep, rows))
-            c = lax.div(start, rows)
-            for i in range(HALF_BLOCKS):
-                du1[i // RING, i % RING, c, v, pl.ds(r, rstep), :] = value[:, i * blk:(i + 1) * blk]
-        layer_rows(u1, 0, 0, total, v, put_du1)
-
-    a2a_recv, a2a_send = new_ids('r', BLOCKS), new_ids('s', BLOCKS)
-
-    slots = (hx, zf, xf1, xf2)
-    per = RING * rows
-
-    turn = (0, 1, 3, PAIR)
-
-    def h_fetch(chunk):
-        at = chunk % RING
-        begin = pl.multiple_of(near['z'][turn[chunk // PAIR]] * per, per)
-        made = [pltpu.make_async_copy((h_a, h_b)[chunk % PAIR].at[pl.ds(begin, per), pl.ds(kh * half, half)],
-                                      slots[at].at[kh], hsem.at[at * PAIR + kh]) for kh in subs]
-        for copy in made:
-            copy.start()
-        return made
-
-    fetches = [h_fetch(chunk) for chunk in range(RING)]
+    a2a_recv, a2a_send = [new_ids('r', BLOCKS) for _ in subs], [new_ids('s', BLOCKS) for _ in subs]
     own_half = lax.div(mid, HALF_BLOCKS)
     self_out = jnp.where(own_half == core, PAIR * (mid - HALF_BLOCKS * core) + core, -1)
     self_in = jnp.where(own_half == core, mid, -1)
-    a2a_home, a2a_sem = a2a.at[zc, yc], rsem.at[a2a_recv[0] + mid]
-
-    def block(k):
-        return du1.at[lax.div(k, HALF_BLOCKS), wrap(lax.div(k, PAIR)), lax.rem(k, PAIR)]
-
-    @pl.loop(0, BLOCKS)
-    def _(k):
-        @pl.when(self_out == k)
-        def _():
-            a2a_home[...] = block(k)[...]
-
-        @pl.when(self_out != k)
-        def _():
-            pltpu.make_async_remote_copy(
-                src_ref=block(k), dst_ref=a2a_home, send_sem=ssem.at[a2a_send[0] + k], recv_sem=a2a_sem,
-                device_id=(HALF_BLOCKS * core + lax.div(k, PAIR), x_base + lax.rem(k, PAIR)),
-                device_id_type=MESH_ID).start()
-
-    plan.work(1)
-    arrived = max([plan.send(axis, 32 * rows * blk, TWO_HOPS) for axis in 'zy'])
-    arrivals = [arrived - off for off in (4, PAIR, 1, 0)]
-    for k in range(RING):
-        plan.pump(arrivals[k])
-        plan.until(arrivals[k])
+
+    def block(k, v):
+        return du1.at[lax.div(k, HALF_BLOCKS), wrap(lax.div(k, PAIR)), lax.rem(k, PAIR), v]
+
+    def spread(v):
+        home, home_sem = a2a.at[zc, yc, v], rsem.at[a2a_recv[v][0] + mid]
+
+        @pl.loop(0, BLOCKS)
+        def _(k):
+            @pl.when(self_out == k)
+            def _():
+                home[...] = block(k, v)[...]
+
+            @pl.when(self_out != k)
+            def _():
+                pltpu.make_async_remote_copy(
+                    src_ref=block(k, v), dst_ref=home, send_sem=ssem.at[a2a_send[v][0] + k], recv_sem=home_sem,
+                    device_id=(HALF_BLOCKS * core + lax.div(k, PAIR), x_base + lax.rem(k, PAIR)),
+                    device_id_type=MESH_ID).start()
+
+    def spread_sent(v):
+        @pl.loop(0, BLOCKS)
+        def _(k):
+            @pl.when(self_out != k)
+            def _():
+                pltpu.make_async_copy(block(k, v), block(k, v), ssem.at[a2a_send[v][0] + k]).wait()
+
+    slots = (hx, zf, xf1, xf2)
+    per = RING * rows
+    turn = (0, 1, 3, PAIR)
+    fetches = {}
+
+    def h_fetch(v, k):
+        begin = pl.multiple_of(near['z'][turn[k]] * per, per)
+        made = [pltpu.make_async_copy((h_a, h_b)[v].at[pl.ds(begin, per), pl.ds(kh * half, half)],
+                                      slots[k].at[kh], hsem.at[k * PAIR + kh]) for kh in subs]
+        for copy in made:
+            copy.start()
+        fetches[v, k] = made
+
+    def dw1_product(v, k):
         zz = near['z'][turn[k]]
+
         @pl.loop(0, RING)
         def _(i):
             @pl.when(self_in != zz * RING + i)
             def _():
-                pltpu.make_async_copy(a2a.at[zz, i], a2a.at[zz, i], rsem.at[a2a_recv[0] + zz * RING + i]).wait()
-        for v in subs:
-            chunk = PAIR * k + v
-            at = chunk % RING
-            for copy in fetches[chunk]:
-                copy.wait()
-            grad = jnp.concatenate([a2a[zz, i, v] for i in range(RING)], axis=0)
-            for kh in subs:
-                for q in range(RING):
-                    res = dot_tn(grad, slots[at][kh, :, q * quad:(q + 1) * quad])
-                    spot = (slice(kh * blk, (kh + 1) * blk), slice(q * quad, (q + 1) * quad))
-                    u2[spot] = res + u2[spot] if chunk else res
-            if chunk < RING:
-                fetches.append(h_fetch(chunk + RING))
-        plan.work(1)
-    @pl.loop(0, BLOCKS)
-    def _(k):
-        @pl.when(self_out != k)
-        def _():
-            pltpu.make_async_copy(block(k), block(k), ssem.at[a2a_send[0] + k]).wait()
+                pltpu.make_async_copy(a2a.at[zz, i, v], a2a.at[zz, i, v],
+                                      rsem.at[a2a_recv[v][0] + zz * RING + i]).wait()
+        for copy in fetches[v, k]:
+            copy.wait()
+        grad = jnp.concatenate([a2a[zz, i, v] for i in range(RING)], axis=0)
+        more = 'dw1' in occurred
+        for kh in subs:
+            for q in range(RING):
+                res = dot_tn(grad, slots[k][kh, :, q * quad:(q + 1) * quad])
+                spot = (slice(kh * blk, (kh + 1) * blk), slice(q * quad, (q + 1) * quad))
+                u2[spot] = res + u2[spot] if more else res
+        occurred.add('dw1')
+
+    def put_du1(rsl, value, v):
+        start = rsl.start - v * vrows
+        r = pl.multiple_of(lax.rem(start, rows), min(rstep, rows))
+        c = lax.div(start, rows)
+        for i in range(HALF_BLOCKS):
+            du1[i // RING, i % RING, c, v, pl.ds(r, rstep), :] = value[:, i * blk:(i + 1) * blk]
+
+    def put_du2(rsl, value, v):
+        duf[core, rsl, :] = value
+
+    def settle_q2():
+        for copy in q2:
+            copy.wait_recv()
+
+    def both_in(name):
+        return lambda: plan.now if all((name, v) in occurred for v in subs) else FAR
+
+    def backward_lane(v):
+        views = ((v, v),)
+        yield after(gather_g, v * 3.0), {}, MM
+        embed_product(v)
+        plan.work(MM)
+        yield after([vec_group]), {}, STEP
+        embed_apply(v)
+        plan.work(0.6)
+        copy = share(dzf, v)
+        yield plan.now + SHARE, {}, MM
+        copy.wait_recv()
+        copy.wait_send()
+        occurred.add(('dz', v))
+        if both_in('dz')() < FAR:
+            plan.add([part3_lane()], start_3, first=True)
+        backward_rowsplit(dzf, wg3, views, layer_emit(u2, 1, 0, PAIR))
+        plan.work(MM)
+        out = []
+        yield from stat_steps(0, v, out)
+        affine_grads(out[0], 0)
+        yield both_in('dz'), {}, STEP
+        layer_rows(u2, 1, PAIR, out[0], v, functools.partial(put_du2, v=v))
+        plan.work(0.6)
+        copy = share(duf, v)
+        occurred.add(('du2', v))
+        if both_in('du2')() < FAR:
+            part2_groups.append(plan.add([part2_lane(hh) for hh in subs], start_2, first=True))
+        yield plan.now + SHARE, {}, MM
+        copy.wait_recv()
+        copy.wait_send()
+        once('q2', settle_q2)
+        backward_colsplit(duf, wg2, wq2, views, layer_emit(u1, 0, 1, 0))
+        plan.work(MM)
+        occurred.add(('dx1', v))
+        yield from stat_steps(1, v, out)
+        affine_grads(out[1], PAIR)
+        layer_rows(u1, 0, 0, out[1], v, functools.partial(put_du1, v=v))
+        spread(v)
+        plan.work(0.6)
+        arrived = max([plan.send(axis, BLOCKS * rows * blk, TWO_HOPS) for axis in 'zy'])
+        early = (PAIR, 1, 0, 0)
+        if 'fetch' not in occurred:
+            yield lambda: FAR if not part2_groups else max(after(part2_groups)(), both_in('dx1')()), {}, NOW
+            if 'fetch' not in occurred:
+                occurred.add('fetch')
+                for k in range(RING):
+                    h_fetch(v, k)
+        for k in range(RING):
+            yield lambda k=k: arrived - early[k] if (v, k) in fetches else FAR, {}, 0.5
+            dw1_product(v, k)
+            plan.work(0.6)
+            if (1 - v, k) not in fetches:
+                h_fetch(1 - v, k)
+        spread_sent(v)
+
+    backward = plan.add([backward_lane(v) for v in subs], first=True)
+    plan.finish(backward)
+    sent(q2 + q3 + qg)
+    dg_send, dg_recv = new_ids('s', 1)[0], new_ids('r', 1)[0]
+    dg_copy = rcopy(dgb.at[core], dgb.at[core], dg_send, dg_recv, peer)
+    dg_copy.start()
 
     x_recv, x_send = new_ids('r', RING), new_ids('s', RING)
 
@@ -1002,7 +1078,7 @@
 
     swap = rcopy(strip(other), strip(PAIR), x_send[0], x_recv[0], peer)
     swap.start()
-    plan.need['x'] = plan.now + 3.0
+    plan.expect(0, plan.now + 3.0, 'x')
     plan.pump(plan.now + PAIR)
     swap.wait_recv()
     swap.wait_send()
@@ -1020,26 +1096,19 @@
     for s in subs:
         out_w[0, core, xc, s] = piece_sum[:, s * blk:(s + 1) * blk].T
     sent(shifts)
-    plan.need['x'] = FAR
+    plan.clear()
     published.append(plan.add([publish(0, s) for s in subs], first=True))
     plan.finish(*scatter_3, *scatter_2)
     plan.finish(*published)
     dg_copy.wait_recv()
     dg_copy.wait_send()
-    w_copy = pltpu.make_async_copy(out_w, dw_out, lsem.at[0])
-    w_copy.start()
     small_out[...] = dgb[...]
-    w_copy.wait()
 
 
 def split_kernel(blk, dw_ref, small_ref, loss_out, dw1_out, dw2_out, dw3_out, dg1_out, db1_out, dg2_out, db2_out,
-                 stage, sem_in, sem_out):
+                 sem_out):
     half = HALF_BLOCKS * blk
     mid = lax.axis_index('model')
-    loads = []
-    for slot in range(3):
-        loads.append(pltpu.make_async_copy(dw_ref.at[slot], stage.at[slot], sem_in.at[slot]))
-        loads[-1].start()
     loss_out[...] = small_ref[0, FIRST:SECOND, half:half + 1] + small_ref[1, FIRST:SECOND, half:half + 1]
     for hh in range(PAIR):
         dg2_out[:, hh * half:(hh + 1) * half] = small_ref[hh, FIRST:SECOND, :half]
@@ -1049,11 +1118,10 @@
     db1_out[...] = small_ref[lax.div(mid, HALF_BLOCKS), 3:4, mcols]
     stores = []
     for slot in range(3):
-        loads[slot].wait()
         for t in range(BLOCKS):
             begin = pl.ds(t * blk, blk)
             dst = (dw1_out.at[begin, :], dw2_out.at[:, begin], dw3_out.at[begin, :])[slot]
-            stores.append(pltpu.make_async_copy(stage.at[slot, t // HALF_BLOCKS, (t // PAIR) % RING, t % PAIR], dst,
+            stores.append(pltpu.make_async_copy(dw_ref.at[slot, t // HALF_BLOCKS, (t // PAIR) % RING, t % PAIR], dst,
                                                 sem_out.at[len(stores)]))
             stores[-1].start()
     for copy in stores:
@@ -1077,12 +1145,11 @@
         pltpu.VMEM((PAIR, 6, RING, PAIR, blk, blk), F32), pltpu.VMEM((PAIR, PAIR, 6, PAIR, blk, blk), F32),
         pltpu.VMEM((PAIR, PAIR, 3, blk, blk), F32),
         pltpu.VMEM((RING, RING, HALF_BLOCKS, blk), F32),
-        pltpu.VMEM((PAIR, 3, RING, RING, half), F32), pltpu.VMEM((RING, RING, half), F32),
+        pltpu.VMEM((PAIR, PAIR, 3, RING, PAIR, half), F32), pltpu.VMEM((RING, RING, half), F32),
         pltpu.VMEM((PAIR, RING, half + blk), F32),
-        pltpu.VMEM((PAIR, RING, half), F32), pltpu.VMEM((RING, RING, HALF_BLOCKS, blk), F32),
+        pltpu.VMEM((PAIR, PAIR, PAIR, half), F32), pltpu.VMEM((RING, RING, HALF_BLOCKS, blk), F32),
         pltpu.VMEM((RING, 40, blk), F32), pltpu.VMEM((PAIR, 40, blk), F32),
         pltpu.VMEM((PAIR, RING, PAIR, PAIR, rows, blk), BF16), pltpu.VMEM((RING, RING, PAIR, rows, blk), BF16),
-        pltpu.VMEM((3,) + bank, F32),
         dma((N_SEND,)), dma((N_RECV,)), dma((BLOCKS,)), dma((HALF_BLOCKS,)), pltpu.SemaphoreType.REGULAR((12,)),
     ]
     anyspec = pl.BlockSpec(memory_space=pl.ANY)
@@ -1091,9 +1158,9 @@
     packed = jax.ShapeDtypeStruct((3,) + bank, F32)
     step_call = pl.pallas_call(
         functools.partial(mega_kernel, (blk, rows, total_rows)),
-        out_shape=[packed, jax.ShapeDtypeStruct((PAIR, RING, half + blk), F32)],
+        out_shape=[pltpu.VMEM((3,) + bank, F32), jax.ShapeDtypeStruct((PAIR, RING, half + blk), F32)],
         in_specs=[anyspec] * 7 + [vmem, vmem, smem],
-        out_specs=[anyspec, vmem],
+        out_specs=[vmem, vmem],
         scratch_shapes=scratch,
         compiler_params=pltpu.CompilerParams(collective_id=0, has_side_effects=True, vmem_limit_bytes=vmem_limit),
         name='barlow_step',
@@ -1106,14 +1173,15 @@
     split_call = pl.pallas_call(
         functools.partial(split_kernel, blk),
         out_shape=[line(1), tall, wide, tall, line(blk), line(blk), line(dim), line(dim)],
-        in_specs=[anyspec, vmem],
+        in_specs=[vmem, vmem],
         out_specs=[vmem, anyspec, anyspec, anyspec, vmem, vmem, vmem, vmem],
-        scratch_shapes=[pltpu.VMEM((3,) + bank, F32), dma((3,)), dma((48,))],
+        scratch_shapes=[dma((48,))],
         name='split_results',
     )
 
     def call(*args):
-        return split_call(*step_call(*args))
+        packed, small = step_call(*args)
+        return split_call(pltpu.with_memory_space_constraint(packed, pltpu.VMEM), small)
 
     return call
 
@@ -1125,7 +1193,7 @@
         group_rows = h_a.shape[0]
         blk = w_three.shape[1]
         rows = group_rows // BLOCKS
-        call = build_call(blk, rows, group_rows * data_size, 67_000_000)
+        call = build_call(blk, rows, group_rows * data_size, 63_700_000)
         outs = call(h_a, h_b, w_one, w_two, w_three, g_one.reshape(1, -1), b_one.reshape(1, -1),
                     g_two.reshape(1, -1), b_two.reshape(1, -1), lam_off)
         loss, dw1, dw2, dw3, dg1, db1, dg2, db2 = outs

time: 296 us -> 286 us (0.966)
  Pallas kernels: 294 us -> 284 us
    pallas_call x2, Pallas kernels: 294 us -> 284 us  [the longest x1 281 us: call(): packed, small = step_call(*args)]
where the time goes in v5:
time: 286 us
  Pallas kernels  284 us (99%)
    pallas_call x1, Pallas kernels, call(): packed, small = step_call(*args)  281 us

profile of v5, /device:TPU:1, one launch (start us, length us, event | category | flops | bytes accessed | tf_op | source)
XLA Modules:
  0.0 285.8 jit_solution(825483098084912180)
XLA Ops:
  1.3 280.9 %barlow_step.1 = (f32[3,2,4,2,128,128]{5,4,3,2,1,0:T(8,128)S(1)}, f32[2,4,1152]{2,1,0:T(4,128)}) custom-call(bf16[2048,2048]{1,0:T(8,128)(2,1)} %h_a.1, bf16[2048,2048]{1,0:T(8,128)(2,1)} %h_b.1, bf16[2048,128]{1,0:T(8,128)(2,1)} %w_one.1, bf16[128,2048]{1,0:T(8,128)(2,1)} %w_two.1, bf16[2048,128]{1,0:T(8,128)(2,1)} %w_three.1, f32[1,128]{1,0:T(1,128)} %bitcast.11, ...), custom_call_target="tpu_custom_call" | custom-call | tf_op jit(solution)/shard_map/barlow_step/pallas_call | solution.py:1183
  282.2 3.4 %split_results.1 = (f32[1,1]{1,0:T(1,128)}, f32[2048,128]{1,0:T(8,128)}, f32[128,2048]{1,0:T(8,128)}, f32[2048,128]{1,0:T(8,128)}, f32[1,128]{1,0:T(1,128)}, /*i...) custom-call(f32[3,2,4,2,128,128]{5,4,3,2,1,0:T(8,128)S(1)} %get-tuple-element.18.dw_ref, ...), custom_call_target="tpu_custom_call" | custom-call | tf_op jit(solution)/shard_map/split_results/pallas_call | solution.py:1184
